TPU v7x, 256 devices: a whole 4x4x8 slice. The times are simulated.
256 devices in a mesh: row: 2 (over y_hi), circ: 16 (over x, y_lo, core), span: 8 (over z).
Axes of the slice: x: 4, y: 4 (y_hi: 2, y_lo: 2; y = y_hi * 2 + y_lo), z: 8, core: 2. Of those that a mesh axis runs over, the one named last changes fastest.
Arguments:
- density: float32 [2, 128, 128, 256], P('row', 'circ', 'span'), may hold values from 0.6 to 1.6
- velocity: float32 [2, 3, 128, 128, 256], P('row', None, 'circ', 'span'), may hold values from -1.2 to 1.2
- pressure: float32 [2, 128, 128, 256], P('row', 'circ', 'span'), may hold values from 0.6 to 1.6
- blade_force: float32 [2, 3, 128, 128, 256], P('row', None, 'circ', 'span'), may hold values from -4 to 4
- offsets: int32 [2], replicated, may hold values from 0 to 127
- weights: float32 [2, 4], replicated, may hold values from 0.1 to 1
Outputs:
- state: float32 [2, 5, 128, 128, 256], P('row', None, 'circ', 'span')
- plane_flux: float32 [2, 2, 5, 128, 128], P('row', None, None, 'circ', 'span')
All inputs are finite; a program needn't handle non-finite values.
Results may differ from a plain program's by a relative error of at most 0.0003.
Values sent between devices are 32-bit elements; how exact they have to be, the bound alone decides.
A program may use at most 64 MiB of HBM per device.

v0:
```python
import jax
import jax.numpy as jnp
from jax import lax
from jax.sharding import PartitionSpec as P

HEAT_RATIO = 1.4
TIME_STEP = 0.04


def from_partner(block, axis, apart):
    count = lax.axis_size(axis)
    route = []
    for low in range(count):
        high = low | 1 << apart
        if high != low and high < count:
            route += [(low, high), (high, low)]
    return lax.ppermute(block, axis, route)


def from_everyone(value, axis):
    copies = jnp.broadcast_to(value, (lax.axis_size(axis), *value.shape))
    return lax.all_to_all(copies, axis, split_axis=0, concat_axis=0, tiled=True)


def joined_along(parts, dim):
    shape = list(parts.shape[1:])
    shape[dim] *= parts.shape[0]
    return jnp.moveaxis(parts, 0, dim).reshape(shape)


def collect(value, axis, dim):
    parts = from_everyone(value, axis)
    return joined_along(parts, dim)


def extended(value, sides, width):
    edges = {}
    for axis, dim in sides:
        devices, length = (lax.axis_size(axis), value.shape[dim])
        up = [(i, (i + 1) % devices) for i in range(devices)]
        last = lax.slice_in_dim(value, length - width, length, axis=dim)
        leading = lax.slice_in_dim(value, 0, width, axis=dim)
        edges[dim] = (
            lax.ppermute(last, axis, up),
            lax.ppermute(leading, axis, [(b, a) for a, b in up]),
        )
    done = []
    for _, dim in sides:
        low, high = edges[dim]
        around = [(width, width) if d in done else (0, 0) for d in range(value.ndim)]
        value = jnp.concatenate([jnp.pad(low, around), value, jnp.pad(high, around)], axis=dim)
        done.append(dim)
    return value


def direction_flux(cells, direction):
    density_here = cells[0]
    momentum = cells[1:4]
    energy = cells[4]
    kinetic = (
        0.5
        * (momentum[0] * momentum[0] + momentum[1] * momentum[1] + momentum[2] * momentum[2])
        / density_here
    )
    pressure_now = (HEAT_RATIO - 1.0) * (energy - kinetic)
    normal = momentum[direction] / density_here
    components = [
        momentum[direction],
        momentum[0] * normal,
        momentum[1] * normal,
        momentum[2] * normal,
        (energy + pressure_now) * normal,
    ]
    components[1 + direction] = components[1 + direction] + pressure_now
    wave_speed = jnp.abs(normal) + jnp.sqrt(HEAT_RATIO * pressure_now / density_here)
    return (jnp.stack(components), wave_speed)


def face_flux(left_state, right_state, direction):
    left_flux, left_speed = direction_flux(left_state, direction)
    right_flux, right_speed = direction_flux(right_state, direction)
    top_speed = jnp.maximum(left_speed, right_speed)
    return 0.5 * (left_flux + right_flux) - 0.5 * top_speed * (right_state - left_state)


def region_step(padded, force, lower_ghost, upper_ghost):
    region = padded[:, 1:-1, 1:-1]
    circ_flux = face_flux(padded[:, :-1, 1:-1], padded[:, 1:, 1:-1], 1)
    span_flux = face_flux(padded[:, 1:-1, :-1], padded[:, 1:-1, 1:], 2)
    axial_row = jnp.concatenate([lower_ghost, region, upper_ghost], 3)
    axial_flux = face_flux(axial_row[..., :-1], axial_row[..., 1:], 0)
    divergence = (
        axial_flux[..., 1:]
        - axial_flux[..., :-1]
        + (circ_flux[:, 1:] - circ_flux[:, :-1])
        + (span_flux[:, :, 1:] - span_flux[:, :, :-1])
    )
    source = jnp.stack(
        [
            jnp.zeros_like(region[0]),
            region[0] * force[0],
            region[0] * force[1],
            region[0] * force[2],
            jnp.sum(region[1:4] * force, axis=0),
        ]
    )
    updated = region - TIME_STEP * divergence + TIME_STEP * source
    return (updated, axial_flux[..., 0], axial_flux[..., -1])


def conserved(density_row, velocity_row, pressure_row):
    momentum = density_row[None] * velocity_row
    energy = pressure_row / (HEAT_RATIO - 1.0) + 0.5 * density_row * jnp.sum(
        velocity_row * velocity_row, axis=0
    )
    return jnp.concatenate([density_row[None], momentum, energy[None]], 0)


def apply_walls(padded, margin, at_hub, at_casing):
    flip_sign = jnp.array([1.0, 1.0, 1.0, -1.0, 1.0], jnp.float32).reshape(5, 1, 1, 1)
    width_total = padded.shape[2]
    hub_mirror = jnp.flip(padded[:, :, margin : 2 * margin], axis=2) * flip_sign
    casing_mirror = (
        jnp.flip(padded[:, :, width_total - 2 * margin : width_total - margin], axis=2) * flip_sign
    )
    hub_part = jnp.where(at_hub, hub_mirror, padded[:, :, :margin])
    casing_part = jnp.where(at_casing, casing_mirror, padded[:, :, width_total - margin :])
    return jnp.concatenate([hub_part, padded[:, :, margin : width_total - margin], casing_part], 2)


def interface(plane_layer, turn_cells, tap_weights, extent):
    partner = from_partner(plane_layer, "row", 0)
    sector_cells = plane_layer.shape[1]
    sectors = lax.axis_size("circ")
    cycle_cells = sector_cells * sectors
    length = sector_cells + 2 * extent
    whole_cycle = collect(partner, "circ", 1)
    doubled = jnp.concatenate([whole_cycle, whole_cycle], 1)
    start = (lax.axis_index("circ") * sector_cells - extent + turn_cells - 1) % cycle_cells
    window = lax.dynamic_slice_in_dim(doubled, start, length + 3, 1)
    ghost_layer = jnp.zeros_like(window[:, :length])
    for tap_index in range(4):
        ghost_layer = (
            ghost_layer + tap_weights[tap_index] * window[:, tap_index : tap_index + length]
        )
    return ghost_layer


def advance(padded, force, extent, row_index, turn_cells, tap_weights):
    circ_total = padded.shape[1]
    span_total = padded.shape[2]
    own_cells = padded[:, extent + 1 : circ_total - extent - 1, 1 : span_total - 1]
    plane_layer = jnp.where(row_index == 0, own_cells[..., -1], own_cells[..., 0])
    ghost_layer = interface(plane_layer, turn_cells, tap_weights, extent)[..., None]
    region = padded[:, 1:-1, 1:-1]
    inlet = jnp.array([1.0, 0.5, 0.0, 0.0, 2.625], jnp.float32).reshape(5, 1, 1, 1)
    lower_ghost = jnp.where(row_index == 0, jnp.broadcast_to(inlet, ghost_layer.shape), ghost_layer)
    upper_ghost = jnp.where(row_index == 0, ghost_layer, region[..., -1:])
    updated, first_face, last_face = region_step(padded, force, lower_ghost, upper_ghost)
    plane = jnp.where(row_index == 0, last_face, first_face)
    return (updated, plane)


def body(density, velocity, pressure, blade_force, offsets, weights):
    cells = conserved(density[0], velocity[0], pressure[0])
    force = blade_force[0]
    sector_cells = cells.shape[1]
    cycle_cells = sector_cells * lax.axis_size("circ")
    row_index = lax.axis_index("row")
    at_hub = lax.axis_index("span") == 0
    at_casing = lax.axis_index("span") == lax.axis_size("span") - 1
    tap_weights = weights / jnp.sum(weights, axis=1, keepdims=True)
    step_count = offsets.shape[0]
    turns = []
    for step_index in range(step_count):
        turn = offsets[step_index]
        turns.append(jnp.where(row_index == 0, turn, (cycle_cells - turn) % cycle_cells))
    planes = []
    for step_index in range(step_count):
        padded = extended(cells, (("circ", 1), ("span", 2)), 1)
        padded = apply_walls(padded, 1, at_hub, at_casing)
        cells, plane = advance(
            padded, force, 0, row_index, turns[step_index], tap_weights[step_index]
        )
        planes.append(plane)
    return (cells[None], jnp.stack(planes)[None])


def solution(mesh):
    placed = (
        P("row", "circ", "span", None),
        P("row", None, "circ", "span", None),
        P("row", "circ", "span", None),
        P("row", None, "circ", "span", None),
        P(),
        P(),
    )
    return jax.shard_map(
        body,
        mesh=mesh,
        in_specs=placed,
        out_specs=(P("row", None, "circ", "span", None), P("row", None, None, "circ", "span")),
        check_vma=False,
    )
```

profile of v0, /device:TPU:1, one launch (start us, length us, event | category | flops | bytes accessed | tf_op | source)
XLA Modules:
  0.0 74.0 jit_solution(16085383685909029191)
XLA Ops:
  0.7 0.9 %copy-done = f32[1,8,16,256]{3,2,1,0:T(8,128)S(1)} copy-done((f32[1,8,16,256]{3,2,1,0:T(8,128)S(1)}, f32[1,8,16,256]{3,2,1,0:T(8,128)}, u32[]{:S(2)}) %copy-start) | copy-done | bytes 131096
  1.5 1.0 %constant_dynamic-update-slice_fusion.7 = f32[5,8,16,256]{3,2,1,0:T(8,128)S(1)} fusion(f32[5,8,16,256]{3,2,1,0:T(8,128)S(1)} %constant_dynamic-update-slice_fusion.8, f32[1,8,16,256]{3,2,1,0:T(8,128)S(1)} %copy-done, f32[1,3,8,16,256]{4,3,2,1,0:T(8,128)} %param.13), kind=kLoop, calls=%fused_computation.236 | loop fusion | flops 32768 | bytes 393216
  2.7 0.8 %copy-done.6 = f32[1,8,16,256]{3,2,1,0:T(8,128)S(1)} copy-done((f32[1,8,16,256]{3,2,1,0:T(8,128)S(1)}, f32[1,8,16,256]{3,2,1,0:T(8,128)}, u32[]{:S(2)}) %copy-start.6) | copy-done | bytes 131096
  3.6 0.8 %copy-done.3 = f32[5,8,16,256]{3,2,1,0:T(8,128)} copy-done((f32[5,8,16,256]{3,2,1,0:T(8,128)}, f32[5,8,16,256]{3,2,1,0:T(8,128)S(1)}, u32[]{:S(2)}) %copy-start.3) | copy-done | bytes 655384
  4.7 3.8 %collective-permute-start = (f32[5,8,16]{2,1,0:T(8,128)S(1)}, f32[5,8,16]{2,1,0:T(8,128)S(1)}, u32[]{:S(2)}, u32[]{:S(2)}) collective-permute-start(f32[5,8,16]{2,1,0:T(8,128)S(1)} %fusion.29), channel_id=1, source_target_pairs={{0,128},{128,0},{1,129},{129,1},{2,130},{130,2},{3,131},{131,3},{4... | collective-permute-start | bytes 7688 | tf_op jit(solution)/shard_map/ppermute | solution.py:17
  8.6 1.3 %collective-permute-start.1 = (f32[5,1,16,256]{3,2,1,0:T(8,128)S(1)}, f32[5,1,16,256]{3,2,1,0:T(8,128)S(1)}, u32[]{:S(2)}, u32[]{:S(2)}) collective-permute-start(f32[5,1,16,256]{3,2,1,0:T(8,128)S(1)} %get-tuple-element.88), channel_id=1, source_target_pairs={{0,8},{8,16},{16,24},{24,32},{32,40},{40,48},{48,56},{56,64},{64,7... | collective-permute-start | bytes 245768 | tf_op jit(solution)/shard_map/ppermute | solution.py:44
  10.0 1.7 %collective-permute-start.3 = (f32[5,8,1,256]{3,1,2,0:T(8,128)S(1)}, f32[5,8,1,256]{3,1,2,0:T(8,128)S(1)}, u32[]{:S(2)}, u32[]{:S(2)}) collective-permute-start(f32[5,8,1,256]{3,1,2,0:T(8,128)S(1)} %copy.631), channel_id=1, source_target_pairs={{0,1},{1,2},{2,3},{3,4},{4,5},{5,6},{6,7},{7,0},{8,9},{9,10},{10,1... | collective-permute-start | bytes 122888 | tf_op jit(solution)/shard_map/ppermute | solution.py:44
  11.7 4.0 %collective-permute-start.4 = (f32[5,8,1,256]{3,1,2,0:T(8,128)S(1)}, f32[5,8,1,256]{3,1,2,0:T(8,128)S(1)}, u32[]{:S(2)}, u32[]{:S(2)}) collective-permute-start(f32[5,8,1,256]{3,1,2,0:T(8,128)S(1)} %copy.633), channel_id=1, source_target_pairs={{1,0},{2,1},{3,2},{4,3},{5,4},{6,5},{7,6},{0,7},{9,8},{10,9},{11,1... | collective-permute-start | bytes 122888 | tf_op jit(solution)/shard_map/ppermute | solution.py:45
  15.7 0.6 constant_dynamic-update-slice_fusion.19
  16.6 0.4 copy.647
  17.0 0.4 copy.636
  17.4 0.7 constant_dynamic-update-slice_fusion.4
  18.0 0.7 fusion.79
  18.7 0.8 %reshape.106 = f32[16,1,640]{2,1,0:T(1,128)} reshape(f32[16,5,8,16]{3,2,1,0:T(8,128)S(1)} %broadcast_in_dim.17) | data formatting | bytes 81920
  19.5 7.3 %all-to-all-start = ((f32[16,1,640]{2,1,0:T(1,128)}), f32[16,1,640]{2,1,0:T(1,128)S(1)}, u32[]{:S(2)}, u32[]{:S(2)}) async-start(f32[16,1,640]{2,1,0:T(1,128)} %reshape.106), calls=%async_computation | async-start | bytes 81920 | tf_op jit(solution)/shard_map/all_to_all | solution.py:22
  26.8 0.6 fusion.80
  29.9 2.8 %all-to-all-done = f32[16,1,640]{2,1,0:T(1,128)S(1)} async-done(((f32[16,1,640]{2,1,0:T(1,128)}), f32[16,1,640]{2,1,0:T(1,128)S(1)}, u32[]{:S(2)}, u32[]{:S(2)}) %all-to-all-start) | async-done | bytes 40992 | tf_op jit(solution)/shard_map/all_to_all | solution.py:22
  32.7 0.5 broadcast.253
  33.2 0.7 reduce.8
  34.2 0.6 copy-done.9
  34.8 2.6 %select_bitcast_fusion.1 = (f32[5,8,16,1]{2,1,0,3:T(8,128)S(1)}, f32[5,8,16]{2,1,0:T(8,128)S(1)}) fusion(f32[5]{0:T(128)S(1)} %copy-done.9, pred[]{:T(512)S(6)} %eq.11, f32[5,11,16]{2,1,0:T(8,128)S(1)} %fusion.54, f32[]{:T(128)} %bitcast.9, f32[]{:T(128)} %bitcast.8, f32[]{:T(128)} %bitcast.7, f32[]{:T(128)} %bitcast.3), kind=kLoop, calls=%fused_computation.291 | loop fusion | flops 5120 | bytes 15397 | tf_op jit(solution)/shard_map/jit(_where)/select_n | solution.py:157
  37.4 0.3 copy.630
  37.9 0.3 copy.629
  38.2 0.3 pad_maximum_fusion.20
  38.6 0.3 multiply_bitcast_fusion.3
  39.2 0.4 multiply_subtract_fusion
  40.5 0.6 copy-done.8
  41.4 0.4 multiply_bitcast_fusion.2
  42.6 0.3 fusion.8
  42.9 0.7 copy-done.4
  43.6 0.5 fusion.21
  44.5 0.6 collective-permute-start.5
  45.3 0.4 copy.648
  45.8 0.4 copy.645
  46.1 0.8 %collective-permute-start.6 = (f32[5,1,16,256]{3,2,1,0:T(8,128)S(1)}, f32[5,1,16,256]{3,2,1,0:T(8,128)S(1)}, u32[]{:S(2)}, u32[]{:S(2)}) collective-permute-start(f32[5,1,16,256]{3,2,1,0:T(8,128)S(1)} %get-tuple-element.80), channel_id=1, source_target_pairs={{0,8},{8,16},{16,24},{24,32},{32,40},{40,48},{48,56},{56,64},{64,7... | collective-permute-start | bytes 245768 | tf_op jit(solution)/shard_map/ppermute | solution.py:44
  47.1 2.7 %collective-permute-start.9 = (f32[5,8,1,256]{3,1,2,0:T(8,128)S(1)}, f32[5,8,1,256]{3,1,2,0:T(8,128)S(1)}, u32[]{:S(2)}, u32[]{:S(2)}) collective-permute-start(f32[5,8,1,256]{3,1,2,0:T(8,128)S(1)} %copy.642), channel_id=1, source_target_pairs={{1,0},{2,1},{3,2},{4,3},{5,4},{6,5},{7,6},{0,7},{9,8},{10,9},{11,1... | collective-permute-start | bytes 122888 | tf_op jit(solution)/shard_map/ppermute | solution.py:45
  49.8 0.8 %reshape.108 = f32[16,1,640]{2,1,0:T(1,128)} reshape(f32[16,5,8,16]{3,2,1,0:T(8,128)S(1)} %broadcast_in_dim.40) | data formatting | bytes 81920
  50.6 7.6 %all-to-all-start.1 = ((f32[16,1,640]{2,1,0:T(1,128)}), f32[16,1,640]{2,1,0:T(1,128)S(1)}, u32[]{:S(2)}, u32[]{:S(2)}) async-start(f32[16,1,640]{2,1,0:T(1,128)} %reshape.108), calls=%async_computation.1 | async-start | bytes 81920 | tf_op jit(solution)/shard_map/all_to_all | solution.py:22
  58.2 5.9 %all-to-all-done.1 = f32[16,1,640]{2,1,0:T(1,128)S(1)} async-done(((f32[16,1,640]{2,1,0:T(1,128)}), f32[16,1,640]{2,1,0:T(1,128)S(1)}, u32[]{:S(2)}, u32[]{:S(2)}) %all-to-all-start.1) | async-done | bytes 40992 | tf_op jit(solution)/shard_map/all_to_all | solution.py:22
  64.1 0.7 reduce.9
  65.0 2.5 %select_bitcast_fusion = (f32[5,8,16,1]{2,1,0,3:T(8,128)S(1)}, f32[5,8,16]{2,1,0:T(8,128)S(1)}) fusion(f32[5]{0:T(128)S(1)} %copy-done.9, pred[]{:T(512)S(6)} %eq.11, f32[5,11,16]{2,1,0:T(8,128)S(1)} %fusion.53, f32[]{:T(128)} %bitcast.26, f32[]{:T(128)} %bitcast.25, f32[]{:T(128)} %bitcast.24, f32[]{:T(128)} %bitcast.20), kind=kLoop, calls=%fused_computation.290 | loop fusion | flops 5120 | bytes 15397 | tf_op jit(solution)/shard_map/jit(_where)/select_n | solution.py:157
  67.5 0.3 copy.639
  67.9 0.3 copy.638
  68.2 0.4 multiply_bitcast_fusion.1
  69.2 0.4 fusion.2
  70.0 0.6 maximum_bitcast_fusion
  71.0 0.4 multiply_bitcast_fusion
  72.6 1.3 %fusion.16 = f32[1,5,8,16,256]{4,3,2,1,0:T(8,128)} fusion(f32[5,8,16,256]{3,2,1,0:T(8,128)S(1)} %fusion.21, f32[5,8,17,256]{3,2,1,0:T(8,128)S(1)} %fusion.5, f32[5,9,16,256]{3,2,1,0:T(8,128)S(1)} %fusion.11, f32[5,8,16,257]{3,2,1,0:T(8,128)S(1)} %fusion.2, f32[5,8,16,256]{3,2,1,0:T(8,128)S(1)} %constant_dynamic-update-slice_fusion.15), kind=kLoop, calls=%fused_computation.83 | loop fusion | flops 1474560 | bytes 5898240 | tf_op jit(solution)/shard_map/broadcast_in_dim | solution.py:186
  (126 shorter events, 6.5 us)
Async XLA Ops:
  0.6 0.9 %copy-start = (f32[1,8,16,256]{3,2,1,0:T(8,128)S(1)}, f32[1,8,16,256]{3,2,1,0:T(8,128)}, u32[]{:S(2)}) copy-start(f32[1,8,16,256]{3,2,1,0:T(8,128)} %param.10) | copy-start | bytes 393220
  0.6 1.9 %copy-start.1 = (f32[1,3,8,16,256]{4,3,2,1,0:T(8,128)S(1)}, f32[1,3,8,16,256]{4,3,2,1,0:T(8,128)}, u32[]{:S(2)}) copy-start(f32[1,3,8,16,256]{4,3,2,1,0:T(8,128)} %param.13) | copy-start | bytes 1179652
  1.5 1.1 %copy-start.5 = (f32[1,3,8,16,256]{4,3,2,1,0:T(8,128)S(1)}, f32[1,3,8,16,256]{4,3,2,1,0:T(8,128)}, u32[]{:S(2)}) copy-start(f32[1,3,8,16,256]{4,3,2,1,0:T(8,128)} %param.11) | copy-start | bytes 1179652
  2.6 0.9 %copy-start.6 = (f32[1,8,16,256]{3,2,1,0:T(8,128)S(1)}, f32[1,8,16,256]{3,2,1,0:T(8,128)}, u32[]{:S(2)}) copy-start(f32[1,8,16,256]{3,2,1,0:T(8,128)} %param.12) | copy-start | bytes 393220
  3.6 0.8 %copy-start.3 = (f32[5,8,16,256]{3,2,1,0:T(8,128)}, f32[5,8,16,256]{3,2,1,0:T(8,128)S(1)}, u32[]{:S(2)}) copy-start(f32[5,8,16,256]{3,2,1,0:T(8,128)S(1)} %get-tuple-element.91) | copy-start | bytes 1966084
  4.7 14.0 %collective-permute-start = (f32[5,8,16]{2,1,0:T(8,128)S(1)}, f32[5,8,16]{2,1,0:T(8,128)S(1)}, u32[]{:S(2)}, u32[]{:S(2)}) collective-permute-start(f32[5,8,16]{2,1,0:T(8,128)S(1)} %fusion.29), channel_id=1, source_target_pairs={{0,128},{128,0},{1,129},{129,1},{2,130},{130,2},{3,131},{131,3},{4... | collective-permute-start | bytes 7688 | tf_op jit(solution)/shard_map/ppermute | solution.py:17
  8.6 31.3 %collective-permute-start.1 = (f32[5,1,16,256]{3,2,1,0:T(8,128)S(1)}, f32[5,1,16,256]{3,2,1,0:T(8,128)S(1)}, u32[]{:S(2)}, u32[]{:S(2)}) collective-permute-start(f32[5,1,16,256]{3,2,1,0:T(8,128)S(1)} %get-tuple-element.88), channel_id=1, source_target_pairs={{0,8},{8,16},{16,24},{24,32},{32,40},{40,48},{48,56},{56,64},{64,7... | collective-permute-start | bytes 245768 | tf_op jit(solution)/shard_map/ppermute | solution.py:44
  9.9 30.0 %collective-permute-start.2 = (f32[5,1,16,256]{3,2,1,0:T(8,128)S(1)}, f32[5,1,16,256]{3,2,1,0:T(8,128)S(1)}, u32[]{:S(2)}, u32[]{:S(2)}) collective-permute-start(f32[5,1,16,256]{3,2,1,0:T(8,128)S(1)} %get-tuple-element.89), channel_id=1, source_target_pairs={{8,0},{16,8},{24,16},{32,24},{40,32},{48,40},{56,48},{64,56},{72,6... | collective-permute-start | bytes 245768 | tf_op jit(solution)/shard_map/ppermute | solution.py:45
  10.0 29.6 %collective-permute-start.3 = (f32[5,8,1,256]{3,1,2,0:T(8,128)S(1)}, f32[5,8,1,256]{3,1,2,0:T(8,128)S(1)}, u32[]{:S(2)}, u32[]{:S(2)}) collective-permute-start(f32[5,8,1,256]{3,1,2,0:T(8,128)S(1)} %copy.631), channel_id=1, source_target_pairs={{0,1},{1,2},{2,3},{3,4},{4,5},{5,6},{6,7},{7,0},{8,9},{9,10},{10,1... | collective-permute-start | bytes 122888 | tf_op jit(solution)/shard_map/ppermute | solution.py:44
  11.7 4.7 %copy-start.7 = (f32[2,4]{1,0:T(2,128)S(1)}, f32[2,4]{1,0:T(2,128)}, u32[]{:S(2)}) copy-start(f32[2,4]{1,0:T(2,128)} %param.15) | copy-start | bytes 100
  11.7 28.0 %collective-permute-start.4 = (f32[5,8,1,256]{3,1,2,0:T(8,128)S(1)}, f32[5,8,1,256]{3,1,2,0:T(8,128)S(1)}, u32[]{:S(2)}, u32[]{:S(2)}) collective-permute-start(f32[5,8,1,256]{3,1,2,0:T(8,128)S(1)} %copy.633), channel_id=1, source_target_pairs={{1,0},{2,1},{3,2},{4,3},{5,4},{6,5},{7,6},{0,7},{9,8},{10,9},{11,1... | collective-permute-start | bytes 122888 | tf_op jit(solution)/shard_map/ppermute | solution.py:45
  19.5 7.3 %copy-start.10 = (s32[2]{0:T(128)S(1)}, s32[2]{0:T(128)}, u32[]{:S(2)}) copy-start(s32[2]{0:T(128)} %param.14) | copy-start | bytes 28
  19.5 13.2 %all-to-all-start = ((f32[16,1,640]{2,1,0:T(1,128)}), f32[16,1,640]{2,1,0:T(1,128)S(1)}, u32[]{:S(2)}, u32[]{:S(2)}) async-start(f32[16,1,640]{2,1,0:T(1,128)} %reshape.106), calls=%async_computation | async-start | bytes 81920 | tf_op jit(solution)/shard_map/all_to_all | solution.py:22
  34.2 0.7 copy-start.9
  40.5 0.7 copy-start.8
  42.5 1.1 %copy-start.4 = (f32[5,8,16,256]{3,2,1,0:T(8,128)S(1)}, f32[5,8,16,256]{3,2,1,0:T(8,128)}, u32[]{:S(2)}) copy-start(f32[5,8,16,256]{3,2,1,0:T(8,128)} %constant_dynamic-update-slice_fusion.4) | copy-start | bytes 1966084
  44.1 1.1 %copy-start.2 = (f32[5,8,16,256]{3,2,1,0:T(8,128)S(1)}, f32[5,8,16,256]{3,2,1,0:T(8,128)}, u32[]{:S(2)}) copy-start(f32[5,8,16,256]{3,2,1,0:T(8,128)} %constant_dynamic-update-slice_fusion.19) | copy-start | bytes 1966084
  44.5 5.2 %collective-permute-start.5 = (f32[5,8,16]{2,1,0:T(8,128)S(1)}, f32[5,8,16]{2,1,0:T(8,128)S(1)}, u32[]{:S(2)}, u32[]{:S(2)}) collective-permute-start(f32[5,8,16]{2,1,0:T(8,128)S(1)} %fusion.28), channel_id=1, source_target_pairs={{0,128},{128,0},{1,129},{129,1},{2,130},{130,2},{3,131},{131,3},{4... | collective-permute-start | bytes 7688 | tf_op jit(solution)/shard_map/ppermute | solution.py:17
  46.1 24.5 %collective-permute-start.6 = (f32[5,1,16,256]{3,2,1,0:T(8,128)S(1)}, f32[5,1,16,256]{3,2,1,0:T(8,128)S(1)}, u32[]{:S(2)}, u32[]{:S(2)}) collective-permute-start(f32[5,1,16,256]{3,2,1,0:T(8,128)S(1)} %get-tuple-element.80), channel_id=1, source_target_pairs={{0,8},{8,16},{16,24},{24,32},{32,40},{40,48},{48,56},{56,64},{64,7... | collective-permute-start | bytes 245768 | tf_op jit(solution)/shard_map/ppermute | solution.py:44
  47.0 23.6 %collective-permute-start.7 = (f32[5,1,16,256]{3,2,1,0:T(8,128)S(1)}, f32[5,1,16,256]{3,2,1,0:T(8,128)S(1)}, u32[]{:S(2)}, u32[]{:S(2)}) collective-permute-start(f32[5,1,16,256]{3,2,1,0:T(8,128)S(1)} %get-tuple-element.81), channel_id=1, source_target_pairs={{8,0},{16,8},{24,16},{32,24},{40,32},{48,40},{56,48},{64,56},{72,6... | collective-permute-start | bytes 245768 | tf_op jit(solution)/shard_map/ppermute | solution.py:45
  47.1 22.8 %collective-permute-start.8 = (f32[5,8,1,256]{3,1,2,0:T(8,128)S(1)}, f32[5,8,1,256]{3,1,2,0:T(8,128)S(1)}, u32[]{:S(2)}, u32[]{:S(2)}) collective-permute-start(f32[5,8,1,256]{3,1,2,0:T(8,128)S(1)} %copy.640), channel_id=1, source_target_pairs={{0,1},{1,2},{2,3},{3,4},{4,5},{5,6},{6,7},{7,0},{8,9},{9,10},{10,1... | collective-permute-start | bytes 122888 | tf_op jit(solution)/shard_map/ppermute | solution.py:44
  47.1 22.8 %collective-permute-start.9 = (f32[5,8,1,256]{3,1,2,0:T(8,128)S(1)}, f32[5,8,1,256]{3,1,2,0:T(8,128)S(1)}, u32[]{:S(2)}, u32[]{:S(2)}) collective-permute-start(f32[5,8,1,256]{3,1,2,0:T(8,128)S(1)} %copy.642), channel_id=1, source_target_pairs={{1,0},{2,1},{3,2},{4,3},{5,4},{6,5},{7,6},{0,7},{9,8},{10,9},{11,1... | collective-permute-start | bytes 122888 | tf_op jit(solution)/shard_map/ppermute | solution.py:45
  50.6 13.5 %all-to-all-start.1 = ((f32[16,1,640]{2,1,0:T(1,128)}), f32[16,1,640]{2,1,0:T(1,128)S(1)}, u32[]{:S(2)}, u32[]{:S(2)}) async-start(f32[16,1,640]{2,1,0:T(1,128)} %reshape.108), calls=%async_computation.1 | async-start | bytes 81920 | tf_op jit(solution)/shard_map/all_to_all | solution.py:22
where the time goes:
time: 74.5 us; the launch traced here: 74 us
  starting transfers between devices  30 us (40%)
  other arithmetic  18.4 us (25%)
  local copies, waits for them, and re-layouts  13 us (17%)
  waiting for transfers between devices  8.66 us (12%)
  between operations  3.94 us (5%)
    all_to_all x2, starting transfers between devices, from_everyone(): return lax.all_to_all(copies, axis, split_axis=0, concat_axis=0, tiled=True)  14.9 us
    all_to_all x2, waiting for transfers between devices, from_everyone(): return lax.all_to_all(copies, axis, split_axis=0, concat_axis=0, tiled=True)  8.63 us
    unnamed x38, local copies, waits for them, and re-layouts  8.12 us
    ppermute x4, starting transfers between devices, extended(): lax.ppermute(leading, axis, [(b, a) for a, b in up])  6.81 us
    select_n x2, other arithmetic, advance(): jnp.where(row_index == 0, jnp.broadcast_to(inlet, ghost_layer.shape), gho...  5.09 us
    ppermute x2, starting transfers between devices, from_partner(): return lax.ppermute(block, axis, route)  4.44 us
    ppermute x4, starting transfers between devices, extended(): lax.ppermute(last, axis, up)  3.87 us
    unnamed x39, other arithmetic  2.32 us
  transfers between devices with their start and end apart: 12, of which 2 were waited for; matrix products, arithmetic and copies ran while one was open for 26% of the time, Pallas kernels for 0%

commit v1 on v0

v1 whole, which is shorter than its diff:
```python
import functools
import math

import jax
import jax.numpy as jnp
from jax import lax
from jax.experimental import pallas as pl
from jax.experimental.pallas import tpu as pltpu
from jax.sharding import PartitionSpec as P

F32 = jnp.float32
MESH = pl.DeviceIdType.MESH
TIME_STEP = 0.04
HALF_STEP = 0.5 * TIME_STEP
LANES = 128
INLET = (1.0, 0.5, 0.0, 0.0, 2.625)
INLET_U = 0.5
INLET_P = 1.0
INLET_SOUND = math.sqrt(1.4)


def derived(cells):
    density, m0, m1, m2, energy = cells
    inverse = 1.0 / density
    u0, u1, u2 = m0 * inverse, m1 * inverse, m2 * inverse
    pressure = 0.4 * (energy - 0.5 * (m0 * u0 + m1 * u1 + m2 * u2))
    sound = jnp.sqrt(1.4 * pressure * inverse)
    return (u0, u1, u2, pressure, sound)


def twice_flux(left, right, direction):
    cells_l, u_l, p_l, a_l = left
    cells_r, u_r, p_r, a_r = right
    speed = jnp.maximum(a_l, a_r)
    up, down = u_l + speed, u_r - speed
    out = [cells_l[j] * up + cells_r[j] * down for j in range(5)]
    out[1 + direction] = out[1 + direction] + (p_l + p_r)
    out[4] = out[4] + (p_l * u_l + p_r * u_r)
    return out


def along(cells, prims, direction):
    normal = prims[direction]
    return (cells, normal, prims[3], jnp.abs(normal) + prims[4])


def source(cells, force):
    return [
        None,
        cells[0] * force[0],
        cells[0] * force[1],
        cells[0] * force[2],
        cells[1] * force[0] + cells[2] * force[1] + cells[3] * force[2],
    ]


def advanced(cells, div, src):
    out = []
    for j in range(5):
        value = cells[j] - HALF_STEP * div[j]
        if src[j] is not None:
            value = value + TIME_STEP * src[j]
        out.append(value)
    return out


def kernel(
    sectors,
    bands,
    dens,
    vel,
    pres,
    forc,
    offs,
    wts,
    out,
    pf_out,
    U,
    W,
    FO,
    SS,
    SR,
    SP,
    TF,
    PS,
    PR0,
    PR1,
    PN,
    OB,
    PF,
    off_s,
    wts_s,
    in_sem,
    out_sem,
    ps_sem,
    pr_sem,
    ns_sem,
    nr_sem,
    hs_sem,
    hr_sem,
):
    row = lax.axis_index("row")
    circ = lax.axis_index("circ")
    span = lax.axis_index("span")
    cd = FO.shape[2]
    cycle = sectors * cd
    c_low, c_high = lax.rem(circ + sectors - 1, sectors), lax.rem(circ + 1, sectors)
    has_low, has_high = span > 0, span < bands - 1
    rotor = row == 0
    half = 1 - row

    barrier = pltpu.get_barrier_semaphore()
    for i in range(sectors):
        q = lax.rem(circ + sectors // 2 + i, sectors)
        pl.semaphore_signal(
            barrier, inc=1, device_id={"row": 1 - row, "circ": q}, device_id_type=MESH
        )
    for q in (c_low, c_high):
        pl.semaphore_signal(barrier, inc=1, device_id={"circ": q}, device_id_type=MESH)

    @pl.when(has_low)
    def _():
        pl.semaphore_signal(barrier, inc=1, device_id={"span": span - 1}, device_id_type=MESH)

    @pl.when(has_high)
    def _():
        pl.semaphore_signal(barrier, inc=1, device_id={"span": span + 1}, device_id_type=MESH)

    own = pl.ds(1, cd)
    PR = (PR0, PR1)
    loads = []

    def load(src, dst):
        copy = pltpu.make_async_copy(src, dst, in_sem.at[len(loads)])
        copy.start()
        loads.append(copy)

    for h in range(2):
        lanes = pl.ds(h * LANES, LANES)
        load(dens.at[0, :, :, lanes], U.at[0, 0, h, own])
        load(vel.at[0, :, :, :, lanes], U.at[0, pl.ds(1, 3), h, own])
        load(pres.at[0, :, :, lanes], U.at[0, 4, h, own])
    state_loads = len(loads)
    for h in range(2):
        load(forc.at[0, :, :, :, pl.ds(h * LANES, LANES)], FO.at[:, h])
    load(offs, off_s)
    load(wts, wts_s)
    for copy in loads[:state_loads]:
        copy.wait()

    lane = lax.broadcasted_iota(jnp.int32, (8, LANES), 1)
    sub = lax.broadcasted_iota(jnp.int32, (8, LANES), 0)
    block = lane // 16

    def conserve(c, _):
        for h in range(2):
            r = U[0, 0, h, c]
            v = [U[0, 1 + d, h, c] for d in range(3)]
            p = U[0, 4, h, c]
            for d in range(3):
                U[0, 1 + d, h, c] = r * v[d]
            U[0, 4, h, c] = p * 2.5 + 0.5 * r * (v[0] * v[0] + v[1] * v[1] + v[2] * v[2])
        return _

    lax.fori_loop(1, cd + 1, conserve, 0)

    def to_tile(line):
        tile = jnp.broadcast_to(line, (8, LANES))
        for bit in (4, 2, 1):
            tile = jnp.where((sub & bit) != 0, pltpu.roll(tile, LANES - 16 * bit, 1), tile)
        return tile

    def end_layers(block_of):
        ends, nexts = [], []
        for turned in (jnp.transpose(b) for b in block_of):
            ends.append(to_tile(jnp.where(rotor, turned[127:128], turned[0:1])))
            nexts.append(to_tile(jnp.where(rotor, turned[126:127], turned[1:2])))
        return ends, nexts

    def packed(tiles):
        out = tiles[0]
        for f in range(1, 5):
            out = jnp.where(block == f, pltpu.roll(tiles[f], 16 * f, 1), out)
        return jnp.where(block < 5, out, 0.0)

    def unpacked(tile, offset=0):
        return [pltpu.roll(tile, (offset - 16 * f) % LANES, 1) for f in range(5)]

    def plane_copies(par):
        copies = []
        for i in range(sectors):
            q = lax.rem(circ + sectors // 2 + i, sectors)
            copies.append(
                pltpu.make_async_remote_copy(
                    src_ref=PS.at[par],
                    dst_ref=PR[par].at[pl.ds(pl.multiple_of(circ * 8, 8), 8)],
                    send_sem=ps_sem.at[par, i],
                    recv_sem=pr_sem.at[par, circ],
                    device_id={"row": 1 - row, "circ": q},
                    device_id_type=MESH,
                )
            )
        return copies

    def plane_arrivals(par):
        return [
            pltpu.make_async_remote_copy(
                src_ref=PS.at[par],
                dst_ref=PR[par].at[pl.ds(q * 8, 8)],
                send_sem=ps_sem.at[par, q],
                recv_sem=pr_sem.at[par, q],
                device_id={"row": 1 - row},
                device_id_type=MESH,
            )
            for q in range(sectors)
        ]

    def to_neighbour(side, src, dst, send_sem, recv_sem):
        where = (
            {"circ": c_high},
            {"circ": c_low},
            {"span": span + 1},
            {"span": span - 1},
        )[side]
        return pltpu.make_async_remote_copy(
            src_ref=src,
            dst_ref=dst,
            send_sem=send_sem,
            recv_sem=recv_sem,
            device_id=where,
            device_id_type=MESH,
        )

    def near_plane(par, side):
        return to_neighbour(
            side, PS.at[par], PN.at[par, side], ns_sem.at[par, side], nr_sem.at[par, side]
        )

    def halo(par, side):
        if side < 2:
            src = U.at[par, :, :, cd if side == 0 else 1]
            dst = U.at[par, :, :, 0 if side == 0 else cd + 1]
        else:
            src, dst = SS.at[par, side - 2], SR.at[par, side - 2]
        return to_neighbour(side, src, dst, hs_sem.at[par, side], hr_sem.at[par, side])

    sends = (None, None, has_high, has_low)
    takes = (None, None, has_low, has_high)

    def guarded(condition, act):
        if condition is None:
            act()
        else:
            pl.when(condition)(act)

    def start_all(make, par):
        for side in range(4):
            guarded(sends[side], lambda side=side: make(par, side).start())

    def take_all(make, par):
        for side in range(4):
            guarded(takes[side], lambda side=side: make(par, side).wait_recv())

    def drain_all(make, par):
        for side in range(4):
            guarded(sends[side], lambda side=side: make(par, side).wait_send())

    def pack_span(par):
        for f in range(5):
            for h in range(2):
                cells = U[par, f, h, own]
                SS[par, 0, f, h] = cells[:, 15]
                SS[par, 1, f, h] = cells[:, 0]

    def mirror_span(par):
        def hub():
            for f in range(5):
                for h in range(2):
                    edge = SS[par, 1, f, h]
                    SR[par, 0, f, h] = -edge if f == 3 else edge

        def casing():
            for f in range(5):
                for h in range(2):
                    edge = SS[par, 0, f, h]
                    SR[par, 1, f, h] = -edge if f == 3 else edge

        pl.when(jnp.logical_not(has_low))(hub)
        pl.when(jnp.logical_not(has_high))(casing)

    def compact_base(par, ends, nexts, force):
        prims = derived(ends)
        near = [PN[par, k] for k in range(4)]
        flip = [-1.0 if f == 3 else 1.0 for f in range(5)]
        c_lo, c_hi = unpacked(near[0]), unpacked(near[1])
        s_lo = unpacked(near[2], -15)
        s_hi = unpacked(near[3], 15)
        below, above, left, right = [], [], [], []
        for f in range(5):
            below.append(jnp.where(sub == 0, c_lo[f][7:8], pltpu.roll(ends[f], 1, 0)))
            above.append(jnp.where(sub == 7, c_hi[f][0:1], pltpu.roll(ends[f], 7, 0)))
            low = jnp.where(has_low, s_lo[f], flip[f] * ends[f])
            left.append(jnp.where(lane == 0, low, pltpu.roll(ends[f], 1, 1)))
            high = jnp.where(has_high, s_hi[f], flip[f] * ends[f])
            right.append(jnp.where(lane == 15, high, pltpu.roll(ends[f], LANES - 1, 1)))

        def whole(cells, direction):
            return along(cells, derived(cells), direction)

        mid = [along(ends, prims, d) for d in range(3)]
        c_up = twice_flux(mid[1], whole(above, 1), 1)
        c_dn = twice_flux(whole(below, 1), mid[1], 1)
        s_up = twice_flux(mid[2], whole(right, 2), 2)
        s_dn = twice_flux(whole(left, 2), mid[2], 2)
        other = [jnp.where(rotor, b, a) for a, b in zip(ends, nexts)]
        inner = [jnp.where(rotor, a, b) for a, b in zip(ends, nexts)]
        axial = twice_flux(whole(other, 0), whole(inner, 0), 0)
        sign = jnp.where(rotor, 1.0, -1.0)
        div = [
            (c_up[j] - c_dn[j]) + (s_up[j] - s_dn[j]) - sign * axial[j] for j in range(5)
        ]
        return advanced(ends, div, source(ends, force))

    def compact_finish(par, ends, base):
        PR[par][pl.ds(cycle, 16)] = PR[par][pl.ds(0, 16)]
        turn = off_s[par]
        turn = jnp.where(rotor, turn, cycle - turn)
        start = lax.rem(circ * cd + turn - 1 + cycle, cycle)
        taps = [jnp.full((8, LANES), wts_s[par, k], F32) for k in range(4)]
        scale = 1.0 / ((taps[0] + taps[1]) + (taps[2] + taps[3]))
        ghost = jnp.zeros((8, LANES), F32)
        for k in range(4):
            ghost = ghost + (taps[k] * scale) * PR[par][pl.ds(start + k, 8), :]
        ghost = unpacked(ghost)
        left = [jnp.where(rotor, a, b) for a, b in zip(ends, ghost)]
        right = [jnp.where(rotor, b, a) for a, b in zip(ends, ghost)]
        plane = twice_flux(
            along(left, derived(left), 0), along(right, derived(right), 0), 0
        )
        for j in range(5):
            PF[par, j] = 0.5 * plane[j][:, :16]
        step = jnp.where(rotor, -HALF_STEP, HALF_STEP)
        return [base[j] + step * plane[j] for j in range(5)]

    def insert(par_tile, dest):
        turned = jnp.transpose(par_tile)
        here = lax.broadcasted_iota(jnp.int32, (16, LANES), 1) == jnp.where(rotor, 127, 0)
        for f in range(5):
            for c in range(cd):
                column = jnp.broadcast_to(turned[16 * f : 16 * f + 16, c : c + 1], (16, LANES))
                dest(f, c, here, column)

    def prim_rows(par, first, last):
        def one(c, _):
            for h in range(2):
                values = derived([U[par, f, h, c] for f in range(5)])
                for k in range(5):
                    W[k, h, c] = values[k]
            return _

        lax.fori_loop(first, last, one, 0)

    lane16 = lax.broadcasted_iota(jnp.int32, (16, LANES), 1)
    sub16 = lax.broadcasted_iota(jnp.int32, (16, LANES), 0)

    def span_edges(par):
        for h in range(2):
            low = [SR[par, 0, f, h] for f in range(5)]
            prims = derived(low)
            SP[0, h] = prims[2]
            SP[1, h] = prims[3]
            SP[2, h] = jnp.abs(prims[2]) + prims[4]
            high = [SR[par, 1, f, h] for f in range(5)]
            mine = [SS[par, 0, f, h] for f in range(5)]
            top = twice_flux(
                along(mine, derived(mine), 2), along(high, derived(high), 2), 2
            )
            for f in range(5):
                TF[f, h] = top[f]

    def bulk(par, store):
        def state_at(c):
            return [
                ([U[par, f, h, c] for f in range(5)], [W[k, h, c] for k in range(5)])
                for h in range(2)
            ]

        def c_faces(low, high):
            return tuple(
                tuple(
                    twice_flux(along(*low[h], 1), along(*high[h], 1), 1) for h in range(2)
                )
            )

        def one(c, lower):
            here = state_at(c + 1)
            upper = c_faces(here, state_at(c + 2))
            div = [[upper[h][j] - lower[h][j] for j in range(5)] for h in range(2)]

            full = [along(*here[h], 0) for h in range(2)]

            def before(pick, inlet):
                turned = [pltpu.roll(pick(full[h]), 1, 1) for h in range(2)]
                return (
                    jnp.where(lane16 == 0, inlet, turned[0]),
                    jnp.where(lane16 == 0, turned[0], turned[1]),
                )

            cells = [before(lambda s, f=f: s[0][f], INLET[f]) for f in range(5)]
            u = before(lambda s: s[1], INLET_U)
            p = before(lambda s: s[2], INLET_P)
            a = before(lambda s: s[3], INLET_U + INLET_SOUND)
            flux = [
                twice_flux(([x[h] for x in cells], u[h], p[h], a[h]), full[h], 0)
                for h in range(2)
            ]
            last = twice_flux(full[1], full[1], 0)
            for j in range(5):
                turned = [pltpu.roll(flux[h][j], LANES - 1, 1) for h in range(2)]
                div[0][j] += jnp.where(lane16 == 127, turned[1], turned[0]) - flux[0][j]
                div[1][j] += jnp.where(lane16 == 127, last[j], turned[1]) - flux[1][j]

            for h in range(2):
                full = along(*here[h], 2)

                def under(value, edge):
                    return jnp.where(sub16 == 0, edge, pltpu.roll(value, 1, 0))

                edge_row = pl.ds(c, 1)
                cells = [
                    under(full[0][f], SR[par, 0, f, h, edge_row, :]) for f in range(5)
                ]
                flux = twice_flux(
                    (
                        cells,
                        under(full[1], SP[0, h, edge_row, :]),
                        under(full[2], SP[1, h, edge_row, :]),
                        under(full[3], SP[2, h, edge_row, :]),
                    ),
                    full,
                    2,
                )
                for j in range(5):
                    above = jnp.where(
                        sub16 == 15, TF[j, h, edge_row, :], pltpu.roll(flux[j], 15, 0)
                    )
                    div[h][j] += above - flux[j]
                force = [FO[d, h, c] for d in range(3)]
                new = advanced(here[h][0], div[h], source(here[h][0], force))
                for j in range(5):
                    store(j, h, c, new[j])
            return upper

        lax.fori_loop(0, cd, one, c_faces(state_at(0), state_at(1)))

    def blocks_of(ref):
        return [ref(f).reshape(cd * 16, LANES) for f in range(5)]

    ends, nexts = end_layers(blocks_of(lambda f: U[0, f, half, own]))
    PS[0] = packed(ends)
    pack_span(0)
    peers = sectors + 2 + has_low.astype(jnp.int32) + has_high.astype(jnp.int32)
    pl.semaphore_wait(barrier, peers)
    sent = plane_copies(0)
    for copy in sent:
        copy.start()
    start_all(near_plane, 0)
    start_all(halo, 0)
    mirror_span(0)
    for copy in loads[state_loads:]:
        copy.wait()
    force, _ = end_layers([FO[d, half].reshape(cd * 16, LANES) for d in range(3)])
    prim_rows(0, 1, cd + 1)
    take_all(near_plane, 0)
    base = compact_base(0, ends, nexts, force)
    take_all(halo, 0)
    prim_rows(0, 0, 1)
    prim_rows(0, cd + 1, cd + 2)
    span_edges(0)

    def keep(j, h, c, value):
        U[1, j, h, c + 1] = value

    bulk(0, keep)
    for copy in plane_arrivals(0):
        copy.wait_recv()
    ends = compact_finish(0, ends, base)
    tile = packed(ends)
    PS[1] = tile
    sent_next = plane_copies(1)
    for copy in sent_next:
        copy.start()
    start_all(near_plane, 1)

    def into_state(f, c, here, column):
        U[1, f, half, c + 1] = jnp.where(here, column, U[1, f, half, c + 1])

    insert(tile, into_state)
    pack_span(1)
    start_all(halo, 1)
    mirror_span(1)

    _, nexts = end_layers(blocks_of(lambda f: U[1, f, half, own]))
    prim_rows(1, 1, cd + 1)
    take_all(near_plane, 1)
    base = compact_base(1, ends, nexts, force)
    take_all(halo, 1)
    prim_rows(1, 0, 1)
    prim_rows(1, cd + 1, cd + 2)
    span_edges(1)

    def emit(j, h, c, value):
        OB[j, h, c] = value

    bulk(1, emit)

    def store_half(h, lane_start, sem):
        return pltpu.make_async_copy(
            OB.at[:, h], out.at[0, :, :, :, pl.ds(lane_start, LANES)], sem
        )

    for copy in plane_arrivals(1):
        copy.wait_recv()
    ends = compact_finish(1, ends, base)

    def into_out(f, c, here, column):
        OB[f, half, c] = jnp.where(here, column, OB[f, half, c])

    insert(packed(ends), into_out)
    writes = [store_half(h, h * LANES, out_sem.at[h]) for h in range(2)]
    writes.append(pltpu.make_async_copy(PF, pf_out.at[0], out_sem.at[2]))
    for copy in writes:
        copy.start()
    for copies in (sent, sent_next):
        for copy in copies:
            copy.wait_send()
    for par in range(2):
        drain_all(near_plane, par)
        drain_all(halo, par)
    for copy in writes:
        copy.wait()


def solution(mesh):
    sectors = mesh.shape["circ"]
    bands = mesh.shape["span"]

    def body(density, velocity, pressure, blade_force, offsets, weights):
        _, cd, sd, axial = density.shape
        vmem, dma = pltpu.VMEM, pltpu.SemaphoreType.DMA
        any_space = pl.BlockSpec(memory_space=pl.ANY)
        return pl.pallas_call(
            functools.partial(kernel, sectors, bands),
            out_shape=(
                jax.ShapeDtypeStruct((1, 5, cd, sd, axial), F32),
                jax.ShapeDtypeStruct((1, 2, 5, cd, sd), F32),
            ),
            in_specs=[any_space] * 6,
            out_specs=(any_space, any_space),
            scratch_shapes=[
                vmem((2, 5, 2, cd + 2, sd, LANES), F32),
                vmem((5, 2, cd + 2, sd, LANES), F32),
                vmem((3, 2, cd, sd, LANES), F32),
                vmem((2, 2, 5, 2, cd, LANES), F32),
                vmem((2, 2, 5, 2, cd, LANES), F32),
                vmem((3, 2, cd, LANES), F32),
                vmem((5, 2, cd, LANES), F32),
                vmem((2, 8, LANES), F32),
                vmem(((sectors + 2) * 8, LANES), F32),
                vmem(((sectors + 2) * 8, LANES), F32),
                vmem((2, 4, 8, LANES), F32),
                vmem((5, 2, cd, sd, LANES), F32),
                vmem((2, 5, cd, sd), F32),
                pltpu.SMEM((2,), jnp.int32),
                pltpu.SMEM((2, 4), F32),
                dma((10,)),
                dma((3,)),
                dma((2, sectors)),
                dma((2, sectors)),
                dma((2, 4)),
                dma((2, 4)),
                dma((2, 4)),
                dma((2, 4)),
            ],
            compiler_params=pltpu.CompilerParams(collective_id=0, has_side_effects=True),
        )(density, velocity, pressure, blade_force, offsets, weights)

    placed = (
        P("row", "circ", "span", None),
        P("row", None, "circ", "span", None),
        P("row", "circ", "span", None),
        P("row", None, "circ", "span", None),
        P(),
        P(),
    )
    return jax.shard_map(
        body,
        mesh=mesh,
        in_specs=placed,
        out_specs=(P("row", None, "circ", "span", None), P("row", None, None, "circ", "span")),
        check_vma=False,
    )
```

time: 74.5 us -> 25.3 us (0.34)
  starting transfers between devices: 30 us -> 0 us
  Pallas kernels: 0 us -> 21.9 us
  other arithmetic: 18.4 us -> 0 us
  local copies, waits for them, and re-layouts: 13 us -> 2.62 us
  waiting for transfers between devices: 8.66 us -> 0 us
  between operations: 3.94 us -> 0.65 us
    pallas_call x0 -> x1, Pallas kernels: none -> 21.9 us  [body(): pl.pallas_call(functools.partial(kernel, sectors, bands), out_shape=(jax....]
    ppermute x10 -> x0, starting transfers between devices: 15.1 us -> none  [the longest x4 6.81 us: extended(): lax.ppermute(leading, axis, [(b, a) for a, b in up])]
    all_to_all x2 -> x0, starting transfers between devices: 14.9 us -> none  [from_everyone(): return lax.all_to_all(copies, axis, split_axis=0, concat_axis=0, tiled=True)]
    all_to_all x2 -> x0, waiting for transfers between devices: 8.63 us -> none  [from_everyone(): return lax.all_to_all(copies, axis, split_axis=0, concat_axis=0, tiled=True)]
    select_n x10 -> x0, other arithmetic: 6.65 us -> none  [the longest x2 5.09 us: advance(): jnp.where(row_index == 0, jnp.broadcast_to(inlet, ghost_layer.shape), gho...]
    unnamed x38 -> x4, local copies, waits for them, and re-layouts: 8.12 us -> 2.62 us
    unnamed x39 -> x0, other arithmetic: 2.32 us -> none
    sub x6 -> x0, other arithmetic: 2.08 us -> none  [face_flux(): 0.5 * (left_flux + right_flux)]
  transfers between devices with their start and end apart: 12 -> 0, of which waited for: 2 -> 0; matrix products, arithmetic and copies ran while one was open for 26% -> 0% of each run, Pallas kernels for 0% -> 0%
where the time goes in v1:
time: 25.3 us; the launch traced here: 25.2 us
  Pallas kernels  21.9 us (87%)
  local copies, waits for them, and re-layouts  2.62 us (10%)
  between operations  0.65 us (3%)
    pallas_call x1, Pallas kernels, body(): pl.pallas_call(functools.partial(kernel, sectors, bands), out_shape=(jax....  21.9 us
    unnamed x4, local copies, waits for them, and re-layouts  2.62 us

profile of v1, /device:TPU:1, one launch (start us, length us, event | category | flops | bytes accessed | tf_op | source)
XLA Modules:
  0.0 25.2 jit_solution(10216363741490511735)
XLA Ops:
  0.6 21.9 %shard_map.77 = (f32[1,5,8,16,256]{4,3,2,1,0:T(8,128)}, f32[1,2,5,8,16]{4,3,2,1,0:T(8,128)}) custom-call(f32[1,8,16,256]{3,2,1,0:T(8,128)} %dens.1, f32[1,3,8,16,256]{4,3,2,1,0:T(8,128)} %vel.1, f32[1,8,16,256]{3,2,1,0:T(8,128)} %pres.1, f32[1,3,8,16,256]{4,3,2,1,0:T(8,128)} %forc.1, s32[2]{0:T(128)} %offs.1, f32[2,4]{1,0:T(2,128)} %wts.1), custom_call_target="tpu_custom_call" | custom-call | tf_op jit(solution)/shard_map/pallas_call | solution.py:552
  22.5 0.0 copy-start
  22.5 2.0 %copy.10 = f32[1,5,8,16,256]{4,3,2,1,0:T(8,128)} copy(f32[1,5,8,16,256]{4,3,2,1,0:T(8,128)} %get-tuple-element.4) | data formatting | bytes 1310720
  24.5 0.0 copy-done
  24.5 0.6 %copy.11 = f32[1,2,5,8,16]{4,3,2,1,0:T(8,128)} copy(f32[1,2,5,8,16]{4,3,2,1,0:T(8,128)S(1)} %copy-done) | data formatting | bytes 10240
Async XLA Ops:
  22.5 2.0 %copy-start = (f32[1,2,5,8,16]{4,3,2,1,0:T(8,128)S(1)}, f32[1,2,5,8,16]{4,3,2,1,0:T(8,128)}, u32[]{:S(2)}) copy-start(f32[1,2,5,8,16]{4,3,2,1,0:T(8,128)} %get-tuple-element.5) | copy-start | bytes 15364

commit v2 on v1

--- a/solution.py
+++ b/solution.py
@@ -73,25 +73,20 @@
     forc,
     offs,
     wts,
-    out,
-    pf_out,
+    OB,
+    PF,
     U,
     W,
     FO,
     SS,
     SR,
-    SP,
-    TF,
     PS,
     PR0,
     PR1,
     PN,
-    OB,
-    PF,
     off_s,
     wts_s,
     in_sem,
-    out_sem,
     ps_sem,
     pr_sem,
     ns_sem,
@@ -135,8 +130,8 @@
         copy.start()
         loads.append(copy)
 
-    for h in range(2):
-        lanes = pl.ds(h * LANES, LANES)
+    for h in (half, row):
+        lanes = pl.ds(pl.multiple_of(h * LANES, LANES), LANES)
         load(dens.at[0, :, :, lanes], U.at[0, 0, h, own])
         load(vel.at[0, :, :, :, lanes], U.at[0, pl.ds(1, 3), h, own])
         load(pres.at[0, :, :, lanes], U.at[0, 4, h, own])
@@ -145,8 +140,6 @@
         load(forc.at[0, :, :, :, pl.ds(h * LANES, LANES)], FO.at[:, h])
     load(offs, off_s)
     load(wts, wts_s)
-    for copy in loads[:state_loads]:
-        copy.wait()
 
     lane = lax.broadcasted_iota(jnp.int32, (8, LANES), 1)
     sub = lax.broadcasted_iota(jnp.int32, (8, LANES), 0)
@@ -161,8 +154,6 @@
                 U[0, 1 + d, h, c] = r * v[d]
             U[0, 4, h, c] = p * 2.5 + 0.5 * r * (v[0] * v[0] + v[1] * v[1] + v[2] * v[2])
         return _
-
-    lax.fori_loop(1, cd + 1, conserve, 0)
 
     def to_tile(line):
         tile = jnp.broadcast_to(line, (8, LANES))
@@ -338,7 +329,7 @@
             along(left, derived(left), 0), along(right, derived(right), 0), 0
         )
         for j in range(5):
-            PF[par, j] = 0.5 * plane[j][:, :16]
+            PF[0, par, j] = 0.5 * plane[j][:, :16]
         step = jnp.where(rotor, -HALF_STEP, HALF_STEP)
         return [base[j] + step * plane[j] for j in range(5)]
 
@@ -363,21 +354,6 @@
     lane16 = lax.broadcasted_iota(jnp.int32, (16, LANES), 1)
     sub16 = lax.broadcasted_iota(jnp.int32, (16, LANES), 0)
 
-    def span_edges(par):
-        for h in range(2):
-            low = [SR[par, 0, f, h] for f in range(5)]
-            prims = derived(low)
-            SP[0, h] = prims[2]
-            SP[1, h] = prims[3]
-            SP[2, h] = jnp.abs(prims[2]) + prims[4]
-            high = [SR[par, 1, f, h] for f in range(5)]
-            mine = [SS[par, 0, f, h] for f in range(5)]
-            top = twice_flux(
-                along(mine, derived(mine), 2), along(high, derived(high), 2), 2
-            )
-            for f in range(5):
-                TF[f, h] = top[f]
-
     def bulk(par, store):
         def state_at(c):
             return [
@@ -385,17 +361,18 @@
                 for h in range(2)
             ]
 
-        def c_faces(low, high):
-            return tuple(
-                tuple(
-                    twice_flux(along(*low[h], 1), along(*high[h], 1), 1) for h in range(2)
+        def one(c, lower, last_row):
+            here = state_at(c + 1)
+            if last_row:
+                upper = None
+                div = [[-lower[h][j] for j in range(5)] for h in range(2)]
+            else:
+                there = state_at(c + 2)
+                upper = tuple(
+                    tuple(twice_flux(along(*here[h], 1), along(*there[h], 1), 1))
+                    for h in range(2)
                 )
-            )
-
-        def one(c, lower):
-            here = state_at(c + 1)
-            upper = c_faces(here, state_at(c + 2))
-            div = [[upper[h][j] - lower[h][j] for j in range(5)] for h in range(2)]
+                div = [[upper[h][j] - lower[h][j] for j in range(5)] for h in range(2)]
 
             full = [along(*here[h], 0) for h in range(2)]
 
@@ -422,42 +399,69 @@
 
             for h in range(2):
                 full = along(*here[h], 2)
-
-                def under(value, edge):
-                    return jnp.where(sub16 == 0, edge, pltpu.roll(value, 1, 0))
-
-                edge_row = pl.ds(c, 1)
-                cells = [
-                    under(full[0][f], SR[par, 0, f, h, edge_row, :]) for f in range(5)
-                ]
                 flux = twice_flux(
                     (
-                        cells,
-                        under(full[1], SP[0, h, edge_row, :]),
-                        under(full[2], SP[1, h, edge_row, :]),
-                        under(full[3], SP[2, h, edge_row, :]),
+                        [pltpu.roll(full[0][f], 1, 0) for f in range(5)],
+                        pltpu.roll(full[1], 1, 0),
+                        pltpu.roll(full[2], 1, 0),
+                        pltpu.roll(full[3], 1, 0),
                     ),
                     full,
                     2,
                 )
                 for j in range(5):
-                    above = jnp.where(
-                        sub16 == 15, TF[j, h, edge_row, :], pltpu.roll(flux[j], 15, 0)
-                    )
-                    div[h][j] += above - flux[j]
+                    inside = jnp.where(sub16 == 0, 0.0, flux[j])
+                    div[h][j] += pltpu.roll(inside, 15, 0) - inside
                 force = [FO[d, h, c] for d in range(3)]
                 new = advanced(here[h][0], div[h], source(here[h][0], force))
                 for j in range(5):
                     store(j, h, c, new[j])
             return upper
 
-        lax.fori_loop(0, cd, one, c_faces(state_at(0), state_at(1)))
+        none = jnp.zeros((16, LANES), F32)
+        start = tuple(tuple(none for _ in range(5)) for _ in range(2))
+        final = lax.fori_loop(0, cd - 1, lambda c, lower: one(c, lower, False), start)
+        one(cd - 1, final, True)
+
+    def edges(par, shift):
+        def flux_of(low, high, direction):
+            return twice_flux(
+                along(low, derived(low), direction),
+                along(high, derived(high), direction),
+                direction,
+            )
+
+        for h in range(2):
+            rows = [[U[par, f, h, c] for f in range(5)] for c in (0, 1, cd, cd + 1)]
+            low = flux_of(rows[0], rows[1], 1)
+            high = flux_of(rows[2], rows[3], 1)
+            for j in range(5):
+                shift(j, h, 0, pl.ds(0, 16), HALF_STEP * low[j])
+                shift(j, h, cd - 1, pl.ds(0, 16), -HALF_STEP * high[j])
+            bottom, top = ([SS[par, k, f, h] for f in range(5)] for k in (1, 0))
+            below, above = ([SR[par, k, f, h] for f in range(5)] for k in (0, 1))
+            low = flux_of(below, bottom, 2)
+            high = flux_of(top, above, 2)
+            for j in range(5):
+                shift(j, h, pl.ds(0, cd), 0, HALF_STEP * low[j])
+                shift(j, h, pl.ds(0, cd), 15, -HALF_STEP * high[j])
 
     def blocks_of(ref):
         return [ref(f).reshape(cd * 16, LANES) for f in range(5)]
 
-    ends, nexts = end_layers(blocks_of(lambda f: U[0, f, half, own]))
+    for copy in loads[:3]:
+        copy.wait()
+    (ends, nexts) = end_layers(blocks_of(lambda f: U[0, f, half, own]))
+
+    def conserved(raw):
+        r, v0, v1, v2, p = raw
+        return [r, r * v0, r * v1, r * v2, p * 2.5 + 0.5 * r * (v0 * v0 + v1 * v1 + v2 * v2)]
+
+    ends, nexts = conserved(ends), conserved(nexts)
     PS[0] = packed(ends)
+    for copy in loads[3:state_loads]:
+        copy.wait()
+    lax.fori_loop(1, cd + 1, conserve, 0)
     pack_span(0)
     peers = sectors + 2 + has_low.astype(jnp.int32) + has_high.astype(jnp.int32)
     pl.semaphore_wait(barrier, peers)
@@ -471,17 +475,13 @@
         copy.wait()
     force, _ = end_layers([FO[d, half].reshape(cd * 16, LANES) for d in range(3)])
     prim_rows(0, 1, cd + 1)
+
+    def keep(j, h, c, value):
+        U[1, j, h, c + 1] = value
+
+    bulk(0, keep)
     take_all(near_plane, 0)
     base = compact_base(0, ends, nexts, force)
-    take_all(halo, 0)
-    prim_rows(0, 0, 1)
-    prim_rows(0, cd + 1, cd + 2)
-    span_edges(0)
-
-    def keep(j, h, c, value):
-        U[1, j, h, c + 1] = value
-
-    bulk(0, keep)
     for copy in plane_arrivals(0):
         copy.wait_recv()
     ends = compact_finish(0, ends, base)
@@ -491,6 +491,13 @@
     for copy in sent_next:
         copy.start()
     start_all(near_plane, 1)
+    take_all(halo, 0)
+
+    def shift_state(j, h, c, s, value):
+        c = pl.ds(1, cd) if isinstance(c, pl.Slice) else c + 1
+        U[1, j, h, c, s] = U[1, j, h, c, s] + value
+
+    edges(0, shift_state)
 
     def into_state(f, c, here, column):
         U[1, f, half, c + 1] = jnp.where(here, column, U[1, f, half, c + 1])
@@ -502,41 +509,44 @@
 
     _, nexts = end_layers(blocks_of(lambda f: U[1, f, half, own]))
     prim_rows(1, 1, cd + 1)
+
+    def emit(j, h, c, value):
+        OB[0, j, c, :, h * LANES : (h + 1) * LANES] = value
+
+    bulk(1, emit)
     take_all(near_plane, 1)
     base = compact_base(1, ends, nexts, force)
     take_all(halo, 1)
-    prim_rows(1, 0, 1)
-    prim_rows(1, cd + 1, cd + 2)
-    span_edges(1)
-
-    def emit(j, h, c, value):
-        OB[j, h, c] = value
-
-    bulk(1, emit)
-
-    def store_half(h, lane_start, sem):
-        return pltpu.make_async_copy(
-            OB.at[:, h], out.at[0, :, :, :, pl.ds(lane_start, LANES)], sem
-        )
-
+
+    def shift_out(j, h, c, s, value):
+        lanes = pl.ds(h * LANES, LANES)
+        OB[0, j, c, s, lanes] = OB[0, j, c, s, lanes] + value
+
+    edges(1, shift_out)
     for copy in plane_arrivals(1):
         copy.wait_recv()
     ends = compact_finish(1, ends, base)
 
     def into_out(f, c, here, column):
-        OB[f, half, c] = jnp.where(here, column, OB[f, half, c])
+        lanes = pl.ds(pl.multiple_of(half * LANES, LANES), LANES)
+        OB[0, f, c, :, lanes] = jnp.where(here, column, OB[0, f, c, :, lanes])
 
     insert(packed(ends), into_out)
-    writes = [store_half(h, h * LANES, out_sem.at[h]) for h in range(2)]
-    writes.append(pltpu.make_async_copy(PF, pf_out.at[0], out_sem.at[2]))
-    for copy in writes:
-        copy.start()
     for copies in (sent, sent_next):
         for copy in copies:
             copy.wait_send()
     for par in range(2):
         drain_all(near_plane, par)
         drain_all(halo, par)
+
+
+def write_out(state, plane, out, plane_out, sems):
+    writes = [
+        pltpu.make_async_copy(state, out, sems.at[0]),
+        pltpu.make_async_copy(plane, plane_out, sems.at[1]),
+    ]
+    for copy in writes:
+        copy.start()
     for copy in writes:
         copy.wait()
 
@@ -549,32 +559,28 @@
         _, cd, sd, axial = density.shape
         vmem, dma = pltpu.VMEM, pltpu.SemaphoreType.DMA
         any_space = pl.BlockSpec(memory_space=pl.ANY)
-        return pl.pallas_call(
+        in_vmem = pl.BlockSpec(memory_space=pltpu.VMEM)
+        results = pl.pallas_call(
             functools.partial(kernel, sectors, bands),
             out_shape=(
-                jax.ShapeDtypeStruct((1, 5, cd, sd, axial), F32),
-                jax.ShapeDtypeStruct((1, 2, 5, cd, sd), F32),
+                vmem((1, 5, cd, sd, axial), F32),
+                vmem((1, 2, 5, cd, sd), F32),
             ),
             in_specs=[any_space] * 6,
-            out_specs=(any_space, any_space),
+            out_specs=(in_vmem, in_vmem),
             scratch_shapes=[
                 vmem((2, 5, 2, cd + 2, sd, LANES), F32),
                 vmem((5, 2, cd + 2, sd, LANES), F32),
                 vmem((3, 2, cd, sd, LANES), F32),
                 vmem((2, 2, 5, 2, cd, LANES), F32),
                 vmem((2, 2, 5, 2, cd, LANES), F32),
-                vmem((3, 2, cd, LANES), F32),
-                vmem((5, 2, cd, LANES), F32),
                 vmem((2, 8, LANES), F32),
                 vmem(((sectors + 2) * 8, LANES), F32),
                 vmem(((sectors + 2) * 8, LANES), F32),
                 vmem((2, 4, 8, LANES), F32),
-                vmem((5, 2, cd, sd, LANES), F32),
-                vmem((2, 5, cd, sd), F32),
                 pltpu.SMEM((2,), jnp.int32),
                 pltpu.SMEM((2, 4), F32),
                 dma((10,)),
-                dma((3,)),
                 dma((2, sectors)),
                 dma((2, sectors)),
                 dma((2, 4)),
@@ -584,6 +590,17 @@
             ],
             compiler_params=pltpu.CompilerParams(collective_id=0, has_side_effects=True),
         )(density, velocity, pressure, blade_force, offsets, weights)
+        results = [pltpu.with_memory_space_constraint(x, pltpu.VMEM) for x in results]
+        return pl.pallas_call(
+            write_out,
+            out_shape=(
+                jax.ShapeDtypeStruct((1, 5, cd, sd, axial), F32),
+                jax.ShapeDtypeStruct((1, 2, 5, cd, sd), F32),
+            ),
+            in_specs=[in_vmem, in_vmem],
+            out_specs=(any_space, any_space),
+            scratch_shapes=[dma((2,))],
+        )(*results)
 
     placed = (
         P("row", "circ", "span", None),

time: 25.3 us -> 19.8 us (0.78)
  Pallas kernels: 21.9 us -> 19.1 us
  local copies, waits for them, and re-layouts: 2.62 us -> 0 us
    pallas_call x1 -> x2, Pallas kernels: 21.9 us -> 19.1 us  [the longest x1 18.2 us: body(): pl.pallas_call(functools.partial(kernel, sectors, bands), out_shape=(vmem...]
    unnamed x4 -> x0, local copies, waits for them, and re-layouts: 2.62 us -> none
where the time goes in v2:
time: 19.8 us; the launch traced here: 19.7 us
  Pallas kernels  19.1 us (96%)
  between operations  0.64 us (3%)
    pallas_call x1, Pallas kernels, body(): pl.pallas_call(functools.partial(kernel, sectors, bands), out_shape=(vmem...  18.2 us
    pallas_call x1, Pallas kernels, body(): pl.pallas_call(write_out, out_shape=(jax.ShapeDtypeStruct((1, 5, cd, sd,...  0.86 us

profile of v2, /device:TPU:1, one launch (start us, length us, event | category | flops | bytes accessed | tf_op | source)
XLA Modules:
  0.0 19.7 jit_solution(12933478020490221295)
XLA Ops:
  0.6 18.2 %shard_map.77 = (f32[1,5,8,16,256]{4,3,2,1,0:T(8,128)S(1)}, f32[1,2,5,8,16]{4,3,2,1,0:T(8,128)S(1)}) custom-call(f32[1,8,16,256]{3,2,1,0:T(8,128)} %dens.1, f32[1,3,8,16,256]{4,3,2,1,0:T(8,128)} %vel.1, f32[1,8,16,256]{3,2,1,0:T(8,128)} %pres.1, f32[1,3,8,16,256]{4,3,2,1,0:T(8,128)} %forc.1, s32[2]{0:T(128)} %offs.1, f32[2,4]{1,0:T(2,128)} %wts.1), custom_call_target="tpu_custom_call" | custom-call | tf_op jit(solution)/shard_map/pallas_call | solution.py:563
  18.8 0.9 %shard_map.78 = (f32[1,5,8,16,256]{4,3,2,1,0:T(8,128)}, f32[1,2,5,8,16]{4,3,2,1,0:T(8,128)}) custom-call(f32[1,5,8,16,256]{4,3,2,1,0:T(8,128)S(1)} %get-tuple-element.4.state, f32[1,2,5,8,16]{4,3,2,1,0:T(8,128)S(1)} %get-tuple-element.5.plane), custom_call_target="tpu_custom_call" | custom-call | tf_op jit(solution)/shard_map/pallas_call | solution.py:594

commit v3 on v2

--- a/solution.py
+++ b/solution.py
@@ -80,6 +80,7 @@
     FO,
     SS,
     SR,
+    SC,
     PS,
     PR0,
     PR1,
@@ -104,6 +105,22 @@
     rotor = row == 0
     half = 1 - row
 
+    own = pl.ds(1, cd)
+    PR = (PR0, PR1)
+
+    def load_half(h, sem):
+        lanes = pl.ds(pl.multiple_of(h * LANES, LANES), LANES)
+        for src, dst in (
+            (dens.at[0, :, :, lanes], U.at[0, 0, h, own]),
+            (vel.at[0, :, :, :, lanes], U.at[0, pl.ds(1, 3), h, own]),
+            (pres.at[0, :, :, lanes], U.at[0, 4, h, own]),
+        ):
+            pltpu.make_async_copy(src, dst, in_sem.at[sem]).start()
+
+    def loaded(ref, sem):
+        pltpu.make_async_copy(ref, ref, in_sem.at[sem]).wait()
+
+    load_half(half, 0)
     barrier = pltpu.get_barrier_semaphore()
     for i in range(sectors):
         q = lax.rem(circ + sectors // 2 + i, sectors)
@@ -121,29 +138,17 @@
     def _():
         pl.semaphore_signal(barrier, inc=1, device_id={"span": span + 1}, device_id_type=MESH)
 
-    own = pl.ds(1, cd)
-    PR = (PR0, PR1)
-    loads = []
-
-    def load(src, dst):
-        copy = pltpu.make_async_copy(src, dst, in_sem.at[len(loads)])
-        copy.start()
-        loads.append(copy)
-
-    for h in (half, row):
-        lanes = pl.ds(pl.multiple_of(h * LANES, LANES), LANES)
-        load(dens.at[0, :, :, lanes], U.at[0, 0, h, own])
-        load(vel.at[0, :, :, :, lanes], U.at[0, pl.ds(1, 3), h, own])
-        load(pres.at[0, :, :, lanes], U.at[0, 4, h, own])
-    state_loads = len(loads)
+    load_half(row, 1)
     for h in range(2):
-        load(forc.at[0, :, :, :, pl.ds(h * LANES, LANES)], FO.at[:, h])
-    load(offs, off_s)
-    load(wts, wts_s)
-
-    lane = lax.broadcasted_iota(jnp.int32, (8, LANES), 1)
-    sub = lax.broadcasted_iota(jnp.int32, (8, LANES), 0)
-    block = lane // 16
+        lanes = pl.ds(h * LANES, LANES)
+        pltpu.make_async_copy(forc.at[0, :, :, :, lanes], FO.at[:, h], in_sem.at[2]).start()
+    load_offsets = pltpu.make_async_copy(offs, off_s, in_sem.at[3])
+    load_weights = pltpu.make_async_copy(wts, wts_s, in_sem.at[4])
+    load_offsets.start()
+    load_weights.start()
+
+    lane = lax.broadcasted_iota(jnp.int32, (5, LANES), 1)
+    sub8 = lax.broadcasted_iota(jnp.int32, (8, LANES), 0)
 
     def conserve(c, _):
         for h in range(2):
@@ -158,24 +163,22 @@
     def to_tile(line):
         tile = jnp.broadcast_to(line, (8, LANES))
         for bit in (4, 2, 1):
-            tile = jnp.where((sub & bit) != 0, pltpu.roll(tile, LANES - 16 * bit, 1), tile)
+            tile = jnp.where((sub8 & bit) != 0, pltpu.roll(tile, LANES - 16 * bit, 1), tile)
         return tile
 
     def end_layers(block_of):
         ends, nexts = [], []
         for turned in (jnp.transpose(b) for b in block_of):
-            ends.append(to_tile(jnp.where(rotor, turned[127:128], turned[0:1])))
-            nexts.append(to_tile(jnp.where(rotor, turned[126:127], turned[1:2])))
+            ends.append(jnp.where(rotor, turned[127:128], turned[0:1]))
+            nexts.append(jnp.where(rotor, turned[126:127], turned[1:2]))
         return ends, nexts
 
-    def packed(tiles):
-        out = tiles[0]
-        for f in range(1, 5):
-            out = jnp.where(block == f, pltpu.roll(tiles[f], 16 * f, 1), out)
-        return jnp.where(block < 5, out, 0.0)
-
-    def unpacked(tile, offset=0):
-        return [pltpu.roll(tile, (offset - 16 * f) % LANES, 1) for f in range(5)]
+    def put_lines(par, lines):
+        for f in range(5):
+            PS[par, f : f + 1] = lines[f]
+
+    def lines_of(stack):
+        return [stack[f : f + 1] for f in range(5)]
 
     def plane_copies(par):
         copies = []
@@ -184,27 +187,24 @@
             copies.append(
                 pltpu.make_async_remote_copy(
                     src_ref=PS.at[par],
-                    dst_ref=PR[par].at[pl.ds(pl.multiple_of(circ * 8, 8), 8)],
-                    send_sem=ps_sem.at[par, i],
-                    recv_sem=pr_sem.at[par, circ],
+                    dst_ref=PR[par].at[circ],
+                    send_sem=ps_sem.at[par],
+                    recv_sem=pr_sem.at[par],
                     device_id={"row": 1 - row, "circ": q},
                     device_id_type=MESH,
                 )
             )
         return copies
 
-    def plane_arrivals(par):
-        return [
-            pltpu.make_async_remote_copy(
-                src_ref=PS.at[par],
-                dst_ref=PR[par].at[pl.ds(q * 8, 8)],
-                send_sem=ps_sem.at[par, q],
-                recv_sem=pr_sem.at[par, q],
-                device_id={"row": 1 - row},
-                device_id_type=MESH,
-            )
-            for q in range(sectors)
-        ]
+    def all_planes(par):
+        return pltpu.make_async_remote_copy(
+            src_ref=PR[par],
+            dst_ref=PR[par],
+            send_sem=ps_sem.at[par],
+            recv_sem=pr_sem.at[par],
+            device_id={"row": 1 - row},
+            device_id_type=MESH,
+        )
 
     def to_neighbour(side, src, dst, send_sem, recv_sem):
         where = (
@@ -224,16 +224,16 @@
 
     def near_plane(par, side):
         return to_neighbour(
-            side, PS.at[par], PN.at[par, side], ns_sem.at[par, side], nr_sem.at[par, side]
+            side, PS.at[par], PN.at[par, side], ns_sem.at[side], nr_sem.at[par, max(side - 1, 0)]
         )
 
     def halo(par, side):
         if side < 2:
-            src = U.at[par, :, :, cd if side == 0 else 1]
+            src = SC.at[side] if par else U.at[par, :, :, cd if side == 0 else 1]
             dst = U.at[par, :, :, 0 if side == 0 else cd + 1]
         else:
             src, dst = SS.at[par, side - 2], SR.at[par, side - 2]
-        return to_neighbour(side, src, dst, hs_sem.at[par, side], hr_sem.at[par, side])
+        return to_neighbour(side, src, dst, hs_sem.at[side], hr_sem.at[par, side])
 
     sends = (None, None, has_high, has_low)
     takes = (None, None, has_low, has_high)
@@ -248,9 +248,22 @@
         for side in range(4):
             guarded(sends[side], lambda side=side: make(par, side).start())
 
-    def take_all(make, par):
+    def take_planes(par):
+        both = pltpu.make_async_remote_copy(
+            src_ref=PN.at[par, pl.ds(0, 2)],
+            dst_ref=PN.at[par, pl.ds(0, 2)],
+            send_sem=ns_sem.at[0],
+            recv_sem=nr_sem.at[par, 0],
+            device_id={"circ": c_low},
+            device_id_type=MESH,
+        )
+        both.wait_recv()
+        for side in (2, 3):
+            guarded(takes[side], lambda side=side: near_plane(par, side).wait_recv())
+
+    def take_halos(par):
         for side in range(4):
-            guarded(takes[side], lambda side=side: make(par, side).wait_recv())
+            guarded(takes[side], lambda side=side: halo(par, side).wait_recv())
 
     def drain_all(make, par):
         for side in range(4):
@@ -281,19 +294,18 @@
 
     def compact_base(par, ends, nexts, force):
         prims = derived(ends)
-        near = [PN[par, k] for k in range(4)]
-        flip = [-1.0 if f == 3 else 1.0 for f in range(5)]
-        c_lo, c_hi = unpacked(near[0]), unpacked(near[1])
-        s_lo = unpacked(near[2], -15)
-        s_hi = unpacked(near[3], 15)
-        below, above, left, right = [], [], [], []
-        for f in range(5):
-            below.append(jnp.where(sub == 0, c_lo[f][7:8], pltpu.roll(ends[f], 1, 0)))
-            above.append(jnp.where(sub == 7, c_hi[f][0:1], pltpu.roll(ends[f], 7, 0)))
-            low = jnp.where(has_low, s_lo[f], flip[f] * ends[f])
-            left.append(jnp.where(lane == 0, low, pltpu.roll(ends[f], 1, 1)))
-            high = jnp.where(has_high, s_hi[f], flip[f] * ends[f])
-            right.append(jnp.where(lane == 15, high, pltpu.roll(ends[f], LANES - 1, 1)))
+        stack = PS[par]
+        c_lo, c_hi, s_lo, s_hi = (PN[par, k] for k in range(4))
+        field = lax.broadcasted_iota(jnp.int32, (5, LANES), 0)
+        mirror = jnp.where(field == 3, -stack, stack)
+        place = lane % 16
+        below = pltpu.roll(jnp.where(lane >= LANES - 16, c_lo, stack), 16, 1)
+        above = pltpu.roll(jnp.where(lane < 16, c_hi, stack), LANES - 16, 1)
+        low = jnp.where(has_low, pltpu.roll(s_lo, LANES - 15, 1), mirror)
+        left = jnp.where(place == 0, low, pltpu.roll(stack, 1, 1))
+        high = jnp.where(has_high, pltpu.roll(s_hi, 15, 1), mirror)
+        right = jnp.where(place == 15, high, pltpu.roll(stack, LANES - 1, 1))
+        below, above, left, right = (lines_of(x) for x in (below, above, left, right))
 
         def whole(cells, direction):
             return along(cells, derived(cells), direction)
@@ -313,32 +325,40 @@
         return advanced(ends, div, source(ends, force))
 
     def compact_finish(par, ends, base):
-        PR[par][pl.ds(cycle, 16)] = PR[par][pl.ds(0, 16)]
         turn = off_s[par]
         turn = jnp.where(rotor, turn, cycle - turn)
         start = lax.rem(circ * cd + turn - 1 + cycle, cycle)
-        taps = [jnp.full((8, LANES), wts_s[par, k], F32) for k in range(4)]
+        taps = [jnp.full((5, LANES), wts_s[par, k], F32) for k in range(4)]
         scale = 1.0 / ((taps[0] + taps[1]) + (taps[2] + taps[3]))
-        ghost = jnp.zeros((8, LANES), F32)
+        ghost = jnp.zeros((5, LANES), F32)
         for k in range(4):
-            ghost = ghost + (taps[k] * scale) * PR[par][pl.ds(start + k, 8), :]
-        ghost = unpacked(ghost)
+            place = start + k
+            sector = lax.rem(place // cd, sectors)
+            back = LANES - 16 * lax.rem(place, cd)
+            turned = lax.rem(back, LANES)
+            first = pltpu.roll(PR[par][sector], turned, 1)
+            second = pltpu.roll(PR[par][lax.rem(sector + 1, sectors)], turned, 1)
+            ghost = ghost + (taps[k] * scale) * jnp.where(lane < back, first, second)
+        ghost = lines_of(ghost)
         left = [jnp.where(rotor, a, b) for a, b in zip(ends, ghost)]
         right = [jnp.where(rotor, b, a) for a, b in zip(ends, ghost)]
         plane = twice_flux(
             along(left, derived(left), 0), along(right, derived(right), 0), 0
         )
         for j in range(5):
-            PF[0, par, j] = 0.5 * plane[j][:, :16]
+            PF[0, par, j] = to_tile(0.5 * plane[j])[:, :16]
         step = jnp.where(rotor, -HALF_STEP, HALF_STEP)
         return [base[j] + step * plane[j] for j in range(5)]
 
-    def insert(par_tile, dest):
-        turned = jnp.transpose(par_tile)
+    def insert(lines, dest):
+        tile = jnp.broadcast_to(lines[0], (8, LANES))
+        for f in range(1, 5):
+            tile = jnp.where(sub8 == f, lines[f], tile)
+        turned = jnp.transpose(tile)
         here = lax.broadcasted_iota(jnp.int32, (16, LANES), 1) == jnp.where(rotor, 127, 0)
         for f in range(5):
             for c in range(cd):
-                column = jnp.broadcast_to(turned[16 * f : 16 * f + 16, c : c + 1], (16, LANES))
+                column = jnp.broadcast_to(turned[16 * c : 16 * c + 16, f : f + 1], (16, LANES))
                 dest(f, c, here, column)
 
     def prim_rows(par, first, last):
@@ -449,8 +469,7 @@
     def blocks_of(ref):
         return [ref(f).reshape(cd * 16, LANES) for f in range(5)]
 
-    for copy in loads[:3]:
-        copy.wait()
+    loaded(U.at[0, :, half, own], 0)
     (ends, nexts) = end_layers(blocks_of(lambda f: U[0, f, half, own]))
 
     def conserved(raw):
@@ -458,54 +477,59 @@
         return [r, r * v0, r * v1, r * v2, p * 2.5 + 0.5 * r * (v0 * v0 + v1 * v1 + v2 * v2)]
 
     ends, nexts = conserved(ends), conserved(nexts)
-    PS[0] = packed(ends)
-    for copy in loads[3:state_loads]:
-        copy.wait()
+    put_lines(0, ends)
+    loaded(U.at[0, :, row, own], 1)
+    loaded(FO, 2)
+    load_offsets.wait()
+    load_weights.wait()
     lax.fori_loop(1, cd + 1, conserve, 0)
     pack_span(0)
+    force, _ = end_layers([FO[d, half].reshape(cd * 16, LANES) for d in range(3)])
+    prim_rows(0, 1, cd + 1)
     peers = sectors + 2 + has_low.astype(jnp.int32) + has_high.astype(jnp.int32)
     pl.semaphore_wait(barrier, peers)
-    sent = plane_copies(0)
-    for copy in sent:
+    for copy in plane_copies(0):
         copy.start()
     start_all(near_plane, 0)
     start_all(halo, 0)
     mirror_span(0)
-    for copy in loads[state_loads:]:
-        copy.wait()
-    force, _ = end_layers([FO[d, half].reshape(cd * 16, LANES) for d in range(3)])
-    prim_rows(0, 1, cd + 1)
 
     def keep(j, h, c, value):
         U[1, j, h, c + 1] = value
 
     bulk(0, keep)
-    take_all(near_plane, 0)
-    base = compact_base(0, ends, nexts, force)
-    for copy in plane_arrivals(0):
-        copy.wait_recv()
-    ends = compact_finish(0, ends, base)
-    tile = packed(ends)
-    PS[1] = tile
-    sent_next = plane_copies(1)
-    for copy in sent_next:
-        copy.start()
-    start_all(near_plane, 1)
-    take_all(halo, 0)
-
     def shift_state(j, h, c, s, value):
         c = pl.ds(1, cd) if isinstance(c, pl.Slice) else c + 1
         U[1, j, h, c, s] = U[1, j, h, c, s] + value
 
-    edges(0, shift_state)
+    def halo_part():
+        take_halos(0)
+        edges(0, shift_state)
+        pack_span(1)
+        for f in range(5):
+            for h in range(2):
+                SC[0, f, h] = U[1, f, h, cd]
+                SC[1, f, h] = U[1, f, h, 1]
+        drain_all(halo, 0)
+        start_all(halo, 1)
+        mirror_span(1)
+
+    pl.when(rotor)(halo_part)
+    take_planes(0)
+    base = compact_base(0, ends, nexts, force)
+    all_planes(0).wait_recv()
+    ends = compact_finish(0, ends, base)
+    put_lines(1, ends)
+    drain_all(near_plane, 0)
+    start_all(near_plane, 1)
+    for copy in plane_copies(1):
+        copy.start()
+    pl.when(jnp.logical_not(rotor))(halo_part)
 
     def into_state(f, c, here, column):
         U[1, f, half, c + 1] = jnp.where(here, column, U[1, f, half, c + 1])
 
-    insert(tile, into_state)
-    pack_span(1)
-    start_all(halo, 1)
-    mirror_span(1)
+    insert(ends, into_state)
 
     _, nexts = end_layers(blocks_of(lambda f: U[1, f, half, own]))
     prim_rows(1, 1, cd + 1)
@@ -514,30 +538,27 @@
         OB[0, j, c, :, h * LANES : (h + 1) * LANES] = value
 
     bulk(1, emit)
-    take_all(near_plane, 1)
-    base = compact_base(1, ends, nexts, force)
-    take_all(halo, 1)
+    take_halos(1)
 
     def shift_out(j, h, c, s, value):
         lanes = pl.ds(h * LANES, LANES)
         OB[0, j, c, s, lanes] = OB[0, j, c, s, lanes] + value
 
     edges(1, shift_out)
-    for copy in plane_arrivals(1):
-        copy.wait_recv()
+    take_planes(1)
+    base = compact_base(1, ends, nexts, force)
+    all_planes(0).wait_send()
+    all_planes(1).wait_send()
+    drain_all(near_plane, 1)
+    drain_all(halo, 1)
+    all_planes(1).wait_recv()
     ends = compact_finish(1, ends, base)
 
     def into_out(f, c, here, column):
         lanes = pl.ds(pl.multiple_of(half * LANES, LANES), LANES)
         OB[0, f, c, :, lanes] = jnp.where(here, column, OB[0, f, c, :, lanes])
 
-    insert(packed(ends), into_out)
-    for copies in (sent, sent_next):
-        for copy in copies:
-            copy.wait_send()
-    for par in range(2):
-        drain_all(near_plane, par)
-        drain_all(halo, par)
+    insert(ends, into_out)
 
 
 def write_out(state, plane, out, plane_out, sems):
@@ -574,18 +595,19 @@
                 vmem((3, 2, cd, sd, LANES), F32),
                 vmem((2, 2, 5, 2, cd, LANES), F32),
                 vmem((2, 2, 5, 2, cd, LANES), F32),
-                vmem((2, 8, LANES), F32),
-                vmem(((sectors + 2) * 8, LANES), F32),
-                vmem(((sectors + 2) * 8, LANES), F32),
-                vmem((2, 4, 8, LANES), F32),
+                vmem((2, 5, 2, sd, LANES), F32),
+                vmem((2, 5, LANES), F32),
+                vmem((sectors, 5, LANES), F32),
+                vmem((sectors, 5, LANES), F32),
+                vmem((2, 4, 5, LANES), F32),
                 pltpu.SMEM((2,), jnp.int32),
                 pltpu.SMEM((2, 4), F32),
-                dma((10,)),
-                dma((2, sectors)),
-                dma((2, sectors)),
-                dma((2, 4)),
-                dma((2, 4)),
-                dma((2, 4)),
+                dma((5,)),
+                dma((2,)),
+                dma((2,)),
+                dma((4,)),
+                dma((2, 3)),
+                dma((4,)),
                 dma((2, 4)),
             ],
             compiler_params=pltpu.CompilerParams(collective_id=0, has_side_effects=True),

time: 19.8 us -> 18.9 us (0.955)
  Pallas kernels: 19.1 us -> 18.2 us
    pallas_call x1, Pallas kernels: 18.2 us -> 17.3 us  [body(): pl.pallas_call(functools.partial(kernel, sectors, bands), out_shape=(vmem...]
where the time goes in v3:
time: 18.9 us; the launch traced here: 18.8 us
  Pallas kernels  18.2 us (96%)
  between operations  0.64 us (3%)
    pallas_call x1, Pallas kernels, body(): pl.pallas_call(functools.partial(kernel, sectors, bands), out_shape=(vmem...  17.3 us
    pallas_call x1, Pallas kernels, body(): pl.pallas_call(write_out, out_shape=(jax.ShapeDtypeStruct((1, 5, cd, sd,...  0.86 us

profile of v3, /device:TPU:1, one launch (start us, length us, event | category | flops | bytes accessed | tf_op | source)
XLA Modules:
  0.0 18.8 jit_solution(16905584504055474957)
XLA Ops:
  0.6 17.3 %shard_map.77 = (f32[1,5,8,16,256]{4,3,2,1,0:T(8,128)S(1)}, f32[1,2,5,8,16]{4,3,2,1,0:T(8,128)S(1)}) custom-call(f32[1,8,16,256]{3,2,1,0:T(8,128)} %dens.1, f32[1,3,8,16,256]{4,3,2,1,0:T(8,128)} %vel.1, f32[1,8,16,256]{3,2,1,0:T(8,128)} %pres.1, f32[1,3,8,16,256]{4,3,2,1,0:T(8,128)} %forc.1, s32[2]{0:T(128)} %offs.1, f32[2,4]{1,0:T(2,128)} %wts.1), custom_call_target="tpu_custom_call" | custom-call | tf_op jit(solution)/shard_map/pallas_call | solution.py:584
  17.9 0.9 %shard_map.78 = (f32[1,5,8,16,256]{4,3,2,1,0:T(8,128)}, f32[1,2,5,8,16]{4,3,2,1,0:T(8,128)}) custom-call(f32[1,5,8,16,256]{4,3,2,1,0:T(8,128)S(1)} %get-tuple-element.4.state, f32[1,2,5,8,16]{4,3,2,1,0:T(8,128)S(1)} %get-tuple-element.5.plane), custom_call_target="tpu_custom_call" | custom-call | tf_op jit(solution)/shard_map/pallas_call | solution.py:616

commit v4 on v3

--- a/solution.py
+++ b/solution.py
@@ -345,10 +345,12 @@
         plane = twice_flux(
             along(left, derived(left), 0), along(right, derived(right), 0), 0
         )
+        step = jnp.where(rotor, -HALF_STEP, HALF_STEP)
+        return plane, [base[j] + step * plane[j] for j in range(5)]
+
+    def put_plane(par, plane):
         for j in range(5):
             PF[0, par, j] = to_tile(0.5 * plane[j])[:, :16]
-        step = jnp.where(rotor, -HALF_STEP, HALF_STEP)
-        return [base[j] + step * plane[j] for j in range(5)]
 
     def insert(lines, dest):
         tile = jnp.broadcast_to(lines[0], (8, LANES))
@@ -505,26 +507,26 @@
     def halo_part():
         take_halos(0)
         edges(0, shift_state)
+        drain_all(halo, 0)
         pack_span(1)
         for f in range(5):
             for h in range(2):
                 SC[0, f, h] = U[1, f, h, cd]
                 SC[1, f, h] = U[1, f, h, 1]
-        drain_all(halo, 0)
         start_all(halo, 1)
         mirror_span(1)
 
-    pl.when(rotor)(halo_part)
     take_planes(0)
     base = compact_base(0, ends, nexts, force)
+    drain_all(near_plane, 0)
     all_planes(0).wait_recv()
-    ends = compact_finish(0, ends, base)
+    plane, ends = compact_finish(0, ends, base)
     put_lines(1, ends)
-    drain_all(near_plane, 0)
     start_all(near_plane, 1)
     for copy in plane_copies(1):
         copy.start()
-    pl.when(jnp.logical_not(rotor))(halo_part)
+    halo_part()
+    put_plane(0, plane)
 
     def into_state(f, c, here, column):
         U[1, f, half, c + 1] = jnp.where(here, column, U[1, f, half, c + 1])
@@ -538,6 +540,8 @@
         OB[0, j, c, :, h * LANES : (h + 1) * LANES] = value
 
     bulk(1, emit)
+    take_planes(1)
+    base = compact_base(1, ends, nexts, force)
     take_halos(1)
 
     def shift_out(j, h, c, s, value):
@@ -545,20 +549,19 @@
         OB[0, j, c, s, lanes] = OB[0, j, c, s, lanes] + value
 
     edges(1, shift_out)
-    take_planes(1)
-    base = compact_base(1, ends, nexts, force)
     all_planes(0).wait_send()
     all_planes(1).wait_send()
     drain_all(near_plane, 1)
     drain_all(halo, 1)
     all_planes(1).wait_recv()
-    ends = compact_finish(1, ends, base)
+    plane, ends = compact_finish(1, ends, base)
 
     def into_out(f, c, here, column):
         lanes = pl.ds(pl.multiple_of(half * LANES, LANES), LANES)
         OB[0, f, c, :, lanes] = jnp.where(here, column, OB[0, f, c, :, lanes])
 
     insert(ends, into_out)
+    put_plane(1, plane)
 
 
 def write_out(state, plane, out, plane_out, sems):

time: 18.9 us -> 18.7 us (0.989)
  Pallas kernels: 18.2 us -> 18 us
where the time goes in v4:
time: 18.7 us; the launch traced here: 18.6 us
  Pallas kernels  18 us (96%)
  between operations  0.64 us (3%)
    pallas_call x1, Pallas kernels, body(): pl.pallas_call(functools.partial(kernel, sectors, bands), out_shape=(vmem...  17.1 us
    pallas_call x1, Pallas kernels, body(): pl.pallas_call(write_out, out_shape=(jax.ShapeDtypeStruct((1, 5, cd, sd,...  0.86 us

profile of v4, /device:TPU:1, one launch (start us, length us, event | category | flops | bytes accessed | tf_op | source)
XLA Modules:
  0.0 18.6 jit_solution(548358463223722931)
XLA Ops:
  0.6 17.1 %shard_map.77 = (f32[1,5,8,16,256]{4,3,2,1,0:T(8,128)S(1)}, f32[1,2,5,8,16]{4,3,2,1,0:T(8,128)S(1)}) custom-call(f32[1,8,16,256]{3,2,1,0:T(8,128)} %dens.1, f32[1,3,8,16,256]{4,3,2,1,0:T(8,128)} %vel.1, f32[1,8,16,256]{3,2,1,0:T(8,128)} %pres.1, f32[1,3,8,16,256]{4,3,2,1,0:T(8,128)} %forc.1, s32[2]{0:T(128)} %offs.1, f32[2,4]{1,0:T(2,128)} %wts.1), custom_call_target="tpu_custom_call" | custom-call | tf_op jit(solution)/shard_map/pallas_call | solution.py:587
  17.8 0.9 %shard_map.78 = (f32[1,5,8,16,256]{4,3,2,1,0:T(8,128)}, f32[1,2,5,8,16]{4,3,2,1,0:T(8,128)}) custom-call(f32[1,5,8,16,256]{4,3,2,1,0:T(8,128)S(1)} %get-tuple-element.4.state, f32[1,2,5,8,16]{4,3,2,1,0:T(8,128)S(1)} %get-tuple-element.5.plane), custom_call_target="tpu_custom_call" | custom-call | tf_op jit(solution)/shard_map/pallas_call | solution.py:619

commit v5 on v4

--- a/solution.py
+++ b/solution.py
@@ -87,12 +87,9 @@
     PN,
     off_s,
     wts_s,
-    in_sem,
-    ps_sem,
+    local_sem,
     pr_sem,
-    ns_sem,
     nr_sem,
-    hs_sem,
     hr_sem,
 ):
     row = lax.axis_index("row")
@@ -115,10 +112,10 @@
             (vel.at[0, :, :, :, lanes], U.at[0, pl.ds(1, 3), h, own]),
             (pres.at[0, :, :, lanes], U.at[0, 4, h, own]),
         ):
-            pltpu.make_async_copy(src, dst, in_sem.at[sem]).start()
+            pltpu.make_async_copy(src, dst, local_sem.at[sem]).start()
 
     def loaded(ref, sem):
-        pltpu.make_async_copy(ref, ref, in_sem.at[sem]).wait()
+        pltpu.make_async_copy(ref, ref, local_sem.at[sem]).wait()
 
     load_half(half, 0)
     barrier = pltpu.get_barrier_semaphore()
@@ -141,9 +138,9 @@
     load_half(row, 1)
     for h in range(2):
         lanes = pl.ds(h * LANES, LANES)
-        pltpu.make_async_copy(forc.at[0, :, :, :, lanes], FO.at[:, h], in_sem.at[2]).start()
-    load_offsets = pltpu.make_async_copy(offs, off_s, in_sem.at[3])
-    load_weights = pltpu.make_async_copy(wts, wts_s, in_sem.at[4])
+        pltpu.make_async_copy(forc.at[0, :, :, :, lanes], FO.at[:, h], local_sem.at[2]).start()
+    load_offsets = pltpu.make_async_copy(offs, off_s, local_sem.at[3])
+    load_weights = pltpu.make_async_copy(wts, wts_s, local_sem.at[4])
     load_offsets.start()
     load_weights.start()
 
@@ -188,7 +185,7 @@
                 pltpu.make_async_remote_copy(
                     src_ref=PS.at[par],
                     dst_ref=PR[par].at[circ],
-                    send_sem=ps_sem.at[par],
+                    send_sem=local_sem.at[par],
                     recv_sem=pr_sem.at[par],
                     device_id={"row": 1 - row, "circ": q},
                     device_id_type=MESH,
@@ -200,7 +197,7 @@
         return pltpu.make_async_remote_copy(
             src_ref=PR[par],
             dst_ref=PR[par],
-            send_sem=ps_sem.at[par],
+            send_sem=local_sem.at[par],
             recv_sem=pr_sem.at[par],
             device_id={"row": 1 - row},
             device_id_type=MESH,
@@ -224,7 +221,7 @@
 
     def near_plane(par, side):
         return to_neighbour(
-            side, PS.at[par], PN.at[par, side], ns_sem.at[side], nr_sem.at[par, max(side - 1, 0)]
+            side, PS.at[par], PN.at[par, side], local_sem.at[2 + side], nr_sem.at[par, max(side - 1, 0)]
         )
 
     def halo(par, side):
@@ -233,7 +230,7 @@
             dst = U.at[par, :, :, 0 if side == 0 else cd + 1]
         else:
             src, dst = SS.at[par, side - 2], SR.at[par, side - 2]
-        return to_neighbour(side, src, dst, hs_sem.at[side], hr_sem.at[par, side])
+        return to_neighbour(side, src, dst, local_sem.at[6 + side], hr_sem.at[par, side])
 
     sends = (None, None, has_high, has_low)
     takes = (None, None, has_low, has_high)
@@ -252,7 +249,7 @@
         both = pltpu.make_async_remote_copy(
             src_ref=PN.at[par, pl.ds(0, 2)],
             dst_ref=PN.at[par, pl.ds(0, 2)],
-            send_sem=ns_sem.at[0],
+            send_sem=local_sem.at[2],
             recv_sem=nr_sem.at[par, 0],
             device_id={"circ": c_low},
             device_id_type=MESH,
@@ -605,12 +602,9 @@
                 vmem((2, 4, 5, LANES), F32),
                 pltpu.SMEM((2,), jnp.int32),
                 pltpu.SMEM((2, 4), F32),
-                dma((5,)),
+                dma((10,)),
                 dma((2,)),
-                dma((2,)),
-                dma((4,)),
                 dma((2, 3)),
-                dma((4,)),
                 dma((2, 4)),
             ],
             compiler_params=pltpu.CompilerParams(collective_id=0, has_side_effects=True),

time: 18.7 us -> 18.7 us (level)
  no operation moved by 1% of the time
where the time goes in v5:
time: 18.7 us; the launch traced here: 18.6 us
  Pallas kernels  17.9 us (96%)
  between operations  0.64 us (3%)
    pallas_call x1, Pallas kernels, body(): pl.pallas_call(functools.partial(kernel, sectors, bands), out_shape=(vmem...  17.1 us
    pallas_call x1, Pallas kernels, body(): pl.pallas_call(write_out, out_shape=(jax.ShapeDtypeStruct((1, 5, cd, sd,...  0.86 us

profile of v5, /device:TPU:1, one launch (start us, length us, event | category | flops | bytes accessed | tf_op | source)
XLA Modules:
  0.0 18.6 jit_solution(7286560122610625028)
XLA Ops:
  0.6 17.1 %shard_map.77 = (f32[1,5,8,16,256]{4,3,2,1,0:T(8,128)S(1)}, f32[1,2,5,8,16]{4,3,2,1,0:T(8,128)S(1)}) custom-call(f32[1,8,16,256]{3,2,1,0:T(8,128)} %dens.1, f32[1,3,8,16,256]{4,3,2,1,0:T(8,128)} %vel.1, f32[1,8,16,256]{3,2,1,0:T(8,128)} %pres.1, f32[1,3,8,16,256]{4,3,2,1,0:T(8,128)} %forc.1, s32[2]{0:T(128)} %offs.1, f32[2,4]{1,0:T(2,128)} %wts.1), custom_call_target="tpu_custom_call" | custom-call | tf_op jit(solution)/shard_map/pallas_call | solution.py:584
  17.7 0.9 %shard_map.78 = (f32[1,5,8,16,256]{4,3,2,1,0:T(8,128)}, f32[1,2,5,8,16]{4,3,2,1,0:T(8,128)}) custom-call(f32[1,5,8,16,256]{4,3,2,1,0:T(8,128)S(1)} %get-tuple-element.4.state, f32[1,2,5,8,16]{4,3,2,1,0:T(8,128)S(1)} %get-tuple-element.5.plane), custom_call_target="tpu_custom_call" | custom-call | tf_op jit(solution)/shard_map/pallas_call | solution.py:613

commit v6 on v5

--- a/solution.py
+++ b/solution.py
@@ -241,8 +241,8 @@
         else:
             pl.when(condition)(act)
 
-    def start_all(make, par):
-        for side in range(4):
+    def start_all(make, par, sides=range(4)):
+        for side in sides:
             guarded(sends[side], lambda side=side: make(par, side).start())
 
     def take_planes(par):
@@ -505,12 +505,13 @@
         take_halos(0)
         edges(0, shift_state)
         drain_all(halo, 0)
-        pack_span(1)
         for f in range(5):
             for h in range(2):
                 SC[0, f, h] = U[1, f, h, cd]
                 SC[1, f, h] = U[1, f, h, 1]
-        start_all(halo, 1)
+        start_all(halo, 1, (0, 1))
+        pack_span(1)
+        start_all(halo, 1, (2, 3))
         mirror_span(1)
 
     take_planes(0)

time: 18.7 us -> 18.7 us (level)
  no operation moved by 1% of the time
where the time goes in v6:
time: 18.7 us; the launch traced here: 18.6 us
  Pallas kernels  17.9 us (96%)
  between operations  0.64 us (3%)
    pallas_call x1, Pallas kernels, body(): pl.pallas_call(functools.partial(kernel, sectors, bands), out_shape=(vmem...  17.1 us
    pallas_call x1, Pallas kernels, body(): pl.pallas_call(write_out, out_shape=(jax.ShapeDtypeStruct((1, 5, cd, sd,...  0.86 us

profile of v6, /device:TPU:1, one launch (start us, length us, event | category | flops | bytes accessed | tf_op | source)
XLA Modules:
  0.0 18.6 jit_solution(7412896018892092917)
XLA Ops:
  0.6 17.1 %shard_map.77 = (f32[1,5,8,16,256]{4,3,2,1,0:T(8,128)S(1)}, f32[1,2,5,8,16]{4,3,2,1,0:T(8,128)S(1)}) custom-call(f32[1,8,16,256]{3,2,1,0:T(8,128)} %dens.1, f32[1,3,8,16,256]{4,3,2,1,0:T(8,128)} %vel.1, f32[1,8,16,256]{3,2,1,0:T(8,128)} %pres.1, f32[1,3,8,16,256]{4,3,2,1,0:T(8,128)} %forc.1, s32[2]{0:T(128)} %offs.1, f32[2,4]{1,0:T(2,128)} %wts.1), custom_call_target="tpu_custom_call" | custom-call | tf_op jit(solution)/shard_map/pallas_call | solution.py:585
  17.7 0.9 %shard_map.78 = (f32[1,5,8,16,256]{4,3,2,1,0:T(8,128)}, f32[1,2,5,8,16]{4,3,2,1,0:T(8,128)}) custom-call(f32[1,5,8,16,256]{4,3,2,1,0:T(8,128)S(1)} %get-tuple-element.4.state, f32[1,2,5,8,16]{4,3,2,1,0:T(8,128)S(1)} %get-tuple-element.5.plane), custom_call_target="tpu_custom_call" | custom-call | tf_op jit(solution)/shard_map/pallas_call | solution.py:614
